TPU v7x, 32 devices: a whole 2x2x4 slice. The times are simulated.
32 devices in a mesh: data: 32 (over z, y, x, core).
Axes of the slice: x: 2, y: 2, z: 4, core: 2. Of those that a mesh axis runs over, the one named last changes fastest.
Arguments:
- grad_attn: bfloat16 [32, 64, 65536], P('data')
- grad_mlp: bfloat16 [32, 32, 262144], P('data')
- grad_wide: bfloat16 [32, 16, 1024], P('data')
- grad_vec: bfloat16 [32, 146, 256], P('data')
- weight_attn: float32 [64, 65536], P(None, 'data')
- weight_mlp: float32 [32, 262144], P(None, 'data')
- weight_wide: float32 [16, 1024], P(None, 'data')
- weight_vec: float32 [146, 256], P(None, 'data')
- mom1_attn: float32 [64, 65536], P(None, 'data')
- mom1_mlp: float32 [32, 262144], P(None, 'data')
- mom1_wide: float32 [16, 1024], P(None, 'data')
- mom1_vec: float32 [146, 256], P(None, 'data')
- mom2_attn: float32 [64, 65536], P(None, 'data')
- mom2_mlp: float32 [32, 262144], P(None, 'data')
- mom2_wide: float32 [16, 1024], P(None, 'data')
- mom2_vec: float32 [146, 256], P(None, 'data')
Outputs:
- output 1: bfloat16 [64, 65536], replicated
- output 2: bfloat16 [32, 262144], replicated
- output 3: bfloat16 [16, 1024], replicated
- output 4: bfloat16 [146, 256], replicated
- output 5: float32 [64, 65536], P(None, 'data')
- output 6: float32 [32, 262144], P(None, 'data')
- output 7: float32 [16, 1024], P(None, 'data')
- output 8: float32 [146, 256], P(None, 'data')
- output 9: float32 [64, 65536], P(None, 'data')
- output 10: float32 [32, 262144], P(None, 'data')
- output 11: float32 [16, 1024], P(None, 'data')
- output 12: float32 [146, 256], P(None, 'data')
- output 13: float32 [64, 65536], P(None, 'data')
- output 14: float32 [32, 262144], P(None, 'data')
- output 15: float32 [16, 1024], P(None, 'data')
- output 16: float32 [146, 256], P(None, 'data')
All inputs are finite; a program needn't handle non-finite values.
Results may differ from a plain program's by a relative error of at most 0.001.
Values are sent between devices in bfloat16 or wider.
A program may use at most 1 GiB of HBM per device.

v0:
```python
import jax
import jax.numpy as jnp
from jax import lax
from jax.sharding import PartitionSpec as P

STEP_NUMBER = 10
LEARN_RATE = 0.04
BETA_FIRST = 0.9
BETA_SECOND = 0.999
EPSILON = 1e-6
WEIGHT_DECAY = 0.01
MAX_NORM = 1.0


def adam_direction(mean_grad, weight, first_moment, second_moment, clip_coef):
    clipped = clip_coef * mean_grad
    new_first = BETA_FIRST * first_moment + (1.0 - BETA_FIRST) * clipped
    new_second = BETA_SECOND * second_moment + (1.0 - BETA_SECOND) * (clipped * clipped)
    update = (new_first / (1.0 - BETA_FIRST ** STEP_NUMBER)) / (jnp.sqrt(new_second / (1.0 - BETA_SECOND ** STEP_NUMBER)) + EPSILON) + WEIGHT_DECAY * weight
    return update, new_first, new_second


def solution(mesh):
    group_size = mesh.shape["data"]
    grad_spec = P("data", None, None)
    shard_spec = P(None, "data")
    full_spec = P(None, None)

    def local_step(*all_banks):
        grad_banks = all_banks[0:4]
        weights = all_banks[4:8]
        firsts = all_banks[8:12]
        seconds = all_banks[12:16]
        mean_grads = []
        for grad_bank in grad_banks:
            row_count = grad_bank.shape[1]
            shard_width = grad_bank.shape[2] // group_size
            by_owner = grad_bank.reshape(row_count, group_size, shard_width)
            received = lax.all_to_all(by_owner, "data", 1, 1, tiled=True)
            mean_grads.append(jnp.sum(received, axis=1, dtype=jnp.float32) / group_size)
        local_square = sum(jnp.sum(mean_grad * mean_grad) for mean_grad in mean_grads)
        clip_coef = jnp.minimum(1.0, MAX_NORM / jnp.sqrt(lax.psum(local_square, "data")))
        results = [adam_direction(mean_grads[bank_index], weights[bank_index], firsts[bank_index], seconds[bank_index], clip_coef) for bank_index in range(4)]
        part_sums = jnp.concatenate([jnp.sum(weight * weight, axis=1) for weight in weights] + [jnp.sum(result[0] * result[0], axis=1) for result in results])
        norm_sums = lax.psum(part_sums, "data")
        tensor_count = norm_sums.shape[0] // 2
        trust_ratios = jnp.sqrt(norm_sums[:tensor_count]) / jnp.sqrt(norm_sums[tensor_count:])
        replicas, new_weights = [], []
        first_row = 0
        for bank_index in range(4):
            row_count = weights[bank_index].shape[0]
            trust_ratio = trust_ratios[first_row:first_row + row_count]
            first_row = first_row + row_count
            new_weight = weights[bank_index] - LEARN_RATE * trust_ratio[:, None] * results[bank_index][0]
            new_weights.append(new_weight)
            replicas.append(lax.all_gather(new_weight.astype(jnp.bfloat16), "data", axis=1, tiled=True))
        return tuple(replicas + new_weights + [result[1] for result in results] + [result[2] for result in results])

    return jax.shard_map(local_step, mesh=mesh, in_specs=(grad_spec,) * 4 + (shard_spec,) * 12, out_specs=(full_spec,) * 4 + (shard_spec,) * 12, check_vma=False)
```

profile of v0, /device:TPU:0, one launch (start us, length us, event | category | flops | bytes accessed | tf_op | source)
XLA Modules:
  0.0 929.9 jit_solution(18013055240920659252)
XLA Ops:
  7.2 0.9 reshape.54
  8.1 0.1 copy.48
  8.2 0.8 reshape.58
  8.9 7.4 all-to-all-start.2
  16.3 1.6 copy.42
  17.9 5.4 all-to-all-done.2
  23.4 2.6 all-to-all-start.3
  26.0 12.3 %copy.45 = bf16[8,8,32,2048]{3,2,1,0:T(8,128)(2,1)} copy(bf16[8,8,32,2048]{3,1,2,0:T(8,128)(2,1)} %bitcast.22) | data formatting | bytes 16777216
  38.2 11.2 %copy.39 = bf16[64,32,2048]{2,0,1:T(8,128)(2,1)} copy(bf16[64,32,2048]{2,1,0:T(8,128)(2,1)} %bitcast.20) | data formatting | bytes 16777216 | tf_op jit(solution)/shard_map/reshape | solution.py:38
  49.5 0.0 all-to-all-done.3
  49.5 6.1 all-to-all-start
  55.6 14.7 %copy.46 = bf16[4,8,32,8192]{3,2,1,0:T(8,128)(2,1)S(1)} copy(bf16[4,8,32,8192]{3,1,2,0:T(8,128)(2,1)} %bitcast.21) | data formatting | bytes 33554432
  70.4 22.2 %copy.40 = bf16[32,32,8192]{2,0,1:T(8,128)(2,1)} copy(bf16[32,32,8192]{2,1,0:T(8,128)(2,1)S(1)} %bitcast.19) | data formatting | bytes 33554432 | tf_op jit(solution)/shard_map/reshape | solution.py:38
  92.6 138.9 %all-to-all-done = bf16[64,32,2048]{2,0,1:T(8,128)(2,1)} async-done(((bf16[64,32,2048]{2,0,1:T(8,128)(2,1)}), bf16[64,32,2048]{2,0,1:T(8,128)(2,1)}, u32[]{:S(2)}, u32[]{:S(2)}) %all-to-all-start) | async-done | bytes 8388640 | tf_op jit(solution)/shard_map/all_to_all | solution.py:39
  231.5 11.9 %all-to-all-start.1 = ((bf16[32,32,8192]{2,0,1:T(8,128)(2,1)}), bf16[32,32,8192]{2,0,1:T(8,128)(2,1)}, u32[]{:S(2)}, u32[]{:S(2)}) async-start(bf16[32,32,8192]{2,0,1:T(8,128)(2,1)} %copy.40), calls=%async_computation.1 | async-start | bytes 33554432 | tf_op jit(solution)/shard_map/all_to_all | solution.py:39
  243.4 0.0 copy-start
  243.4 0.0 all-gather.4.cloned.1.call-start
  243.4 0.1 reshape.59
  243.6 0.6 multiply_reduce_fusion.9
  244.2 0.6 multiply_reduce_fusion.8
  244.9 0.0 copy-start.12
  244.9 0.0 copy-start.13
  244.9 5.6 convert_reduce_fusion.1
  250.5 0.7 multiply_reduce_fusion.4
  251.2 341.1 %all-to-all-done.1 = bf16[32,32,8192]{2,0,1:T(8,128)(2,1)} async-done(((bf16[32,32,8192]{2,0,1:T(8,128)(2,1)}), bf16[32,32,8192]{2,0,1:T(8,128)(2,1)}, u32[]{:S(2)}, u32[]{:S(2)}) %all-to-all-start.1) | async-done | bytes 16777248 | tf_op jit(solution)/shard_map/all_to_all | solution.py:39
  592.4 6.8 convert_reduce_fusion
  599.1 0.9 multiply_reduce_fusion.1
  602.6 54.4 %psum.14 = f32[]{:T(128)} all-reduce(f32[]{:T(128)S(6)} %add.75), channel_id=1, replica_groups=mesh['data'=32] {'data'}, use_global_device_ids=true, to_apply=%region_12.0 | all-reduce | flops 1 | bytes 8 | tf_op jit(solution)/shard_map/psum | solution.py:42
  657.7 0.0 copy-done
  657.7 3.8 multiply_reduce_fusion
  661.6 0.0 copy-done.1
  661.6 1.8 multiply_reduce_fusion.3
  663.3 0.0 copy-done.7
  663.3 0.0 copy-done.10
  663.4 0.0 copy-done.11
  663.4 0.0 copy-start.2
  663.4 0.0 copy-start.3
  663.4 0.1 multiply_reduce_fusion.7
  663.6 0.0 copy-start.8
  663.6 0.0 copy-start.9
  663.6 0.0 copy-start.5
  663.6 0.0 copy-start.6
  663.6 0.1 concatenate.3
  663.7 42.2 %psum.15 = f32[516]{0:T(1024)S(1)} all-reduce(f32[516]{0:T(1024)S(1)} %concatenate.3), channel_id=1, replica_groups=mesh['data'=32] {'data'}, use_global_device_ids=true, to_apply=%region_17.0 | all-reduce | flops 516 | bytes 4128 | tf_op jit(solution)/shard_map/psum | solution.py:45
  705.9 0.1 rsqrt_multiply_fusion
  706.0 1.2 fusion.2
  707.2 0.0 all-gather.4.cloned.1.call-update
  707.2 0.3 all-gather.6.cloned.1.call-start
  707.5 0.1 slice_multiply_fusion.2
  707.6 3.3 fusion.1
  710.8 0.0 all-gather.6.cloned.1.call-update
  710.8 0.1 slice_multiply_fusion
  710.9 0.6 fusion
  711.5 40.5 %all_gather.15 = bf16[146,256]{0,1:T(8,128)(2,1)S(1)} all-gather(bf16[146,8]{0,1:T(8,128)(2,1)S(1)} %get-tuple-element.88), channel_id=1, replica_groups=mesh['data'=32] {'data'}, dimensions={1}, use_global_device_ids=true | all-gather | bytes 77088 | tf_op jit(solution)/shard_map/all_gather | solution.py:56
  752.0 0.7 copy.44
  752.8 0.1 slice_multiply_fusion.1
  752.8 0.7 convert_bitcast_fusion
  753.5 37.4 %all-gather = bf16[32,32,16]{1,2,0:T(8,128)(2,1)S(1)} all-gather(bf16[1,32,16]{1,2,0:T(8,128)(2,1)S(1)} %get-tuple-element.90), channel_id=1, replica_groups=mesh['data'=32] {'data'}, dimensions={0}, use_global_device_ids=true | all-gather | bytes 33792 | tf_op jit(solution)/shard_map/all_gather | solution.py:56
  791.0 0.8 reshape.57
  791.8 110.1 %all-gather.6.cloned.1.call-done = bf16[32,262144]{1,0:T(8,128)(2,1)} async-done(((bf16[32,8192]{1,0:T(8,128)(2,1)}), bf16[32,262144]{1,0:T(8,128)(2,1)}) %all-gather.6.cloned.1.call-update) | async-done | bytes 16777232 | tf_op jit(solution)/shard_map/all_gather | solution.py:56
  901.9 7.3 copy.51
  909.2 13.8 %copy.52 = bf16[32,262144]{1,0:T(8,128)(2,1)} copy(bf16[32,262144]{1,0:T(8,128)(2,1)} %all-gather.6.cloned.1.call-done) | data formatting | bytes 33554432
  923.0 0.0 copy-done.2
  923.0 0.0 copy-done.8
  (18 shorter events, 0.2 us)
Async XLA Ops:
  8.9 14.5 %all-to-all-start.2 = ((bf16[32,2,256]{2,1,0:T(2,128)(2,1)}), bf16[32,2,256]{2,1,0:T(2,128)(2,1)S(1)}, u32[]{:S(2)}, u32[]{:S(2)}) async-start(bf16[32,2,256]{2,1,0:T(2,128)(2,1)} %reshape.58), calls=%async_computation.2 | async-start | bytes 65536 | tf_op jit(solution)/shard_map/all_to_all | solution.py:39
  23.4 26.1 %all-to-all-start.3 = ((bf16[146,32,8]{0,2,1:T(8,128)(2,1)}), bf16[146,32,8]{0,2,1:T(8,128)(2,1)S(1)}, u32[]{:S(2)}, u32[]{:S(2)}) async-start(bf16[146,32,8]{0,2,1:T(8,128)(2,1)} %bitcast), calls=%async_computation.3 | async-start | bytes 262144 | tf_op jit(solution)/shard_map/all_to_all | solution.py:39
  49.5 182.0 %all-to-all-start = ((bf16[64,32,2048]{2,0,1:T(8,128)(2,1)}), bf16[64,32,2048]{2,0,1:T(8,128)(2,1)}, u32[]{:S(2)}, u32[]{:S(2)}) async-start(bf16[64,32,2048]{2,0,1:T(8,128)(2,1)} %copy.39), calls=%async_computation | async-start | bytes 16777216 | tf_op jit(solution)/shard_map/all_to_all | solution.py:39
  231.5 360.9 %all-to-all-start.1 = ((bf16[32,32,8192]{2,0,1:T(8,128)(2,1)}), bf16[32,32,8192]{2,0,1:T(8,128)(2,1)}, u32[]{:S(2)}, u32[]{:S(2)}) async-start(bf16[32,32,8192]{2,0,1:T(8,128)(2,1)} %copy.40), calls=%async_computation.1 | async-start | bytes 33554432 | tf_op jit(solution)/shard_map/all_to_all | solution.py:39
  243.4 414.4 %copy-start = (f32[32,8192]{1,0:T(8,128)S(1)}, f32[32,8192]{1,0:T(8,128)}, u32[]{:S(2)}) copy-start(f32[32,8192]{1,0:T(8,128)} %param.21) | copy-start | bytes 3145732
  243.4 548.4 %all-gather.4.cloned.1.call-start = ((), (), s32[]{:S(2)}) async-start(), calls=%async_computation.4 | async-start | bytes 8650752 | tf_op jit(solution)/shard_map/all_gather | solution.py:56
  244.8 416.7 %copy-start.1 = (f32[64,2048]{1,0:T(8,128)S(1)}, f32[64,2048]{1,0:T(8,128)}, u32[]{:S(2)}) copy-start(f32[64,2048]{1,0:T(8,128)} %param.20) | copy-start | bytes 1572868
  244.8 418.5 %copy-start.7 = (f32[16,32]{1,0:T(8,128)S(1)}, f32[16,32]{1,0:T(8,128)}, u32[]{:S(2)}) copy-start(f32[16,32]{1,0:T(8,128)} %param.22) | copy-start | bytes 6148
  244.8 418.5 %copy-start.10 = (f32[16,32]{1,0:T(8,128)S(1)}, f32[16,32]{1,0:T(8,128)}, u32[]{:S(2)}) copy-start(f32[16,32]{1,0:T(8,128)} %param.26) | copy-start | bytes 6148
  244.9 418.5 %copy-start.11 = (f32[16,32]{1,0:T(8,128)S(1)}, f32[16,32]{1,0:T(8,128)}, u32[]{:S(2)}) copy-start(f32[16,32]{1,0:T(8,128)} %param.30) | copy-start | bytes 6148
  244.9 418.7 %copy-start.4 = (f32[146,8]{0,1:T(8,128)S(1)}, f32[146,8]{0,1:T(8,128)}, u32[]{:S(2)}) copy-start(f32[146,8]{0,1:T(8,128)} %param.23) | copy-start | bytes 14020
  244.9 418.7 %copy-start.12 = (f32[146,8]{0,1:T(8,128)S(1)}, f32[146,8]{0,1:T(8,128)}, u32[]{:S(2)}) copy-start(f32[146,8]{0,1:T(8,128)} %param.27) | copy-start | bytes 14020
  244.9 418.7 %copy-start.13 = (f32[146,8]{0,1:T(8,128)S(1)}, f32[146,8]{0,1:T(8,128)}, u32[]{:S(2)}) copy-start(f32[146,8]{0,1:T(8,128)} %param.31) | copy-start | bytes 14020
  663.4 259.6 %copy-start.2 = (f32[64,2048]{1,0:T(8,128)}, f32[64,2048]{1,0:T(8,128)S(1)}, u32[]{:S(2)}) copy-start(f32[64,2048]{1,0:T(8,128)S(1)} %get-tuple-element.128) | copy-start | bytes 1572868
  663.4 259.6 %copy-start.3 = (f32[64,2048]{1,0:T(8,128)}, f32[64,2048]{1,0:T(8,128)S(1)}, u32[]{:S(2)}) copy-start(f32[64,2048]{1,0:T(8,128)S(1)} %get-tuple-element.132) | copy-start | bytes 1572868
  663.6 259.5 %copy-start.8 = (f32[16,32]{1,0:T(8,128)}, f32[16,32]{1,0:T(8,128)S(1)}, u32[]{:S(2)}) copy-start(f32[16,32]{1,0:T(8,128)S(1)} %get-tuple-element.130) | copy-start | bytes 6148
  663.6 259.5 %copy-start.9 = (f32[16,32]{1,0:T(8,128)}, f32[16,32]{1,0:T(8,128)S(1)}, u32[]{:S(2)}) copy-start(f32[16,32]{1,0:T(8,128)S(1)} %get-tuple-element.134) | copy-start | bytes 6148
  663.6 259.4 %copy-start.5 = (f32[146,8]{0,1:T(8,128)}, f32[146,8]{0,1:T(8,128)S(1)}, u32[]{:S(2)}) copy-start(f32[146,8]{0,1:T(8,128)S(1)} %get-tuple-element.131) | copy-start | bytes 14020
  663.6 259.4 %copy-start.6 = (f32[146,8]{0,1:T(8,128)}, f32[146,8]{0,1:T(8,128)S(1)}, u32[]{:S(2)}) copy-start(f32[146,8]{0,1:T(8,128)S(1)} %get-tuple-element.135) | copy-start | bytes 14020
  707.2 194.7 %all-gather.6.cloned.1.call-start = ((), (), s32[]{:S(2)}) async-start(), calls=%async_computation.5 | async-start | bytes 17301504 | tf_op jit(solution)/shard_map/all_gather | solution.py:56
Sparse Core Ops, SparseCore 0:
  707.3 77.7 all-gather.3
  788.6 113.2 all-gather.5
where the time goes:
time: 931 us; the launch traced here: 930 us
  waiting for transfers between devices  596 us (64%)
  blocking collectives  175 us (19%)
  local copies, waits for them, and re-layouts  86.8 us (9%)
  starting transfers between devices  28.3 us (3%)
  other arithmetic  27.1 us (3%)
  between operations  17.6 us (2%)
    all_to_all x4, waiting for transfers between devices, local_step(): received = lax.all_to_all(by_owner, 'data', 1, 1, tiled=True)  485 us
    all_gather x2, waiting for transfers between devices, local_step(): lax.all_gather(new_weight.astype(jnp.bfloat16), 'data', axis=1, tiled=True)  110 us
    all_gather x2, blocking collectives, local_step(): lax.all_gather(new_weight.astype(jnp.bfloat16), 'data', axis=1, tiled=True)  77.9 us
    psum x1, blocking collectives, local_step(): lax.psum(local_square, 'data')  54.4 us
    unnamed x37, local copies, waits for them, and re-layouts  52.2 us
    psum x1, blocking collectives, local_step(): norm_sums = lax.psum(part_sums, 'data')  42.2 us
    reshape x4, local copies, waits for them, and re-layouts, local_step(): by_owner = grad_bank.reshape(row_count, group_size, shard_width)  34.4 us
    all_to_all x4, starting transfers between devices, local_step(): received = lax.all_to_all(by_owner, 'data', 1, 1, tiled=True)  28 us
  transfers between devices with their start and end apart: 6, of which 4 were waited for; matrix products, arithmetic and copies ran while one was open for 8% of the time, Pallas kernels for 0%

commit v1 on v0

v1 whole, which is shorter than its diff:
```python
import jax
import jax.numpy as jnp
from jax import lax
from jax.experimental import pallas as pl
from jax.experimental.pallas import tpu as pltpu
from jax.sharding import PartitionSpec as P

STEP_NUMBER = 10
LEARN_RATE = 0.04
BETA_FIRST = 0.9
BETA_SECOND = 0.999
EPSILON = 1e-6
WEIGHT_DECAY = 0.01
MAX_NORM = 1.0

GROUP = 32
AXIS = "data"
MESH = pl.DeviceIdType.MESH
F32 = jnp.float32
BF16 = jnp.bfloat16

ROWS = 16
WIDTH = 1024
OWN_A = 2048
OWN_M = 8192
SUB_A = OWN_A // WIDTH
SUB_M = OWN_M // WIDTH
CHUNKS_A = 4 * SUB_A
CHUNKS_M = 2 * SUB_M
CHUNKS = CHUNKS_A + CHUNKS_M
PAIRS = CHUNKS // 2
AHEAD = 2
SLOTS = 3
TILES = WIDTH // 128


def coords():
    me = lax.axis_index(AXIS)
    return me // 8, lax.rem(me // 4, 2), lax.rem(me // 2, 2), lax.rem(me, 2)


def index_of(z, y, x, c):
    return ((z * 2 + y) * 2 + x) * 2 + c


def remote(src, dst, send_sem, recv_sem, device):
    return pltpu.make_async_remote_copy(src_ref=src, dst_ref=dst, send_sem=send_sem, recv_sem=recv_sem, device_id=(device,), device_id_type=MESH)


def wait_bytes(ref, sem):
    pltpu.make_async_copy(ref, ref, sem).wait()


def bank_of(k, attn_case, mlp_case):
    @pl.when(k < CHUNKS_A)
    def _():
        attn_case(k // SUB_A, lax.rem(k, SUB_A))

    @pl.when(k >= CHUNKS_A)
    def _():
        local = k - CHUNKS_A
        mlp_case(local // SUB_M, lax.rem(local, SUB_M))


def row_group(k):
    return jnp.where(k < CHUNKS_A, k // SUB_A, 4 + (k - CHUNKS_A) // SUB_M)


def adam(gs, w, m, v, clip):
    clipped = clip * gs
    new_m = BETA_FIRST * m + (1.0 - BETA_FIRST) * clipped
    new_v = BETA_SECOND * v + (1.0 - BETA_SECOND) * (clipped * clipped)
    u = (new_m / (1.0 - BETA_FIRST ** STEP_NUMBER)) / (jnp.sqrt(new_v / (1.0 - BETA_SECOND ** STEP_NUMBER)) + EPSILON) + WEIGHT_DECAY * w
    return u, new_m, new_v


def all_to_all_small(me, start_one):
    def body(i, carry):
        start_one(lax.rem(me + 1 + i, GROUP))
        return carry
    lax.fori_loop(0, GROUP - 1, body, 0)


def step_kernel(g_attn, g_mlp, g_small, w_attn, w_mlp, m_attn, m_mlp, v_attn, v_mlp, w_small, m_small, v_small,
                land, nw, nm, nv, small_all, nw_small, nm_small, nv_small,
                acc1, s2buf, s3buf, gsum, small_in, small_u, msg, inbox1, inbox2, rows_w, rows_u, ratio, clip_tile, n_acc,
                s1_send, s1_recv, s2_send, s2_recv, s3_send, s3_recv, d_send, d_recv, load_sem, misc_send, misc_recv):
    me = lax.axis_index(AXIS)
    z, y, x, c = coords()

    def load_state(k, carry):
        def attn(rg, sub):
            for i, (src, dst) in enumerate(((w_attn, nw), (m_attn, nm), (v_attn, nv))):
                pltpu.make_async_copy(src.at[pl.ds(rg * ROWS, ROWS), pl.ds(pl.multiple_of(sub * WIDTH, 128), WIDTH)], dst.at[k], load_sem.at[i]).start()

        def mlp(rg, sub):
            for i, (src, dst) in enumerate(((w_mlp, nw), (m_mlp, nm), (v_mlp, nv))):
                pltpu.make_async_copy(src.at[pl.ds(rg * ROWS, ROWS), pl.ds(pl.multiple_of(sub * WIDTH, 128), WIDTH)], dst.at[k], load_sem.at[i]).start()
        bank_of(k, attn, mlp)
        return carry
    lax.fori_loop(0, CHUNKS, load_state, 0)

    barrier = pltpu.get_barrier_semaphore()
    all_to_all_small(me, lambda i: pl.semaphore_signal(barrier, inc=1, device_id=(i,), device_id_type=MESH))
    pl.semaphore_wait(barrier, GROUP - 1)

    def a_peer(t, da, dc):
        cc = c + dc - 2 * c * dc
        if t == 0:
            return index_of(z, y, x + da - 2 * x * da, cc)
        return index_of(z, y + da - 2 * y * da, x, cc)

    def b_peer(t):
        return index_of(z, 1 - y, x, c) if t == 0 else index_of(z, y, 1 - x, c)

    def a_of(t):
        return x if t == 0 else y

    def b_of(t):
        return y if t == 0 else x

    def first_start(j, t):
        k = 2 * j + t

        def issue(grad, rg, sub, own):
            def body(b, carry):
                bb, zz = b // 4, lax.rem(b, 4)
                for da in range(2):
                    for dc in range(2):
                        aa = a_of(t) + da - 2 * a_of(t) * da
                        cc = c + dc - 2 * c * dc
                        owner = index_of(zz, bb, aa, cc) if t == 0 else index_of(zz, aa, bb, cc)
                        src = grad.at[0, pl.ds(rg * ROWS, ROWS), pl.ds(pl.multiple_of(owner * own + sub * WIDTH, 128), WIDTH)]
                        dst = land.at[k, (da * 2 + dc) * 8 + b]
                        if da == 0 and dc == 0:
                            pltpu.make_async_copy(src, dst, s1_recv.at[k]).start()
                        else:
                            remote(src, dst, s1_send.at[k], s1_recv.at[k], a_peer(t, da, dc)).start()
                return carry
            lax.fori_loop(0, 8, body, 0)
        bank_of(k, lambda rg, sub: issue(g_attn, rg, sub, OWN_A), lambda rg, sub: issue(g_mlp, rg, sub, OWN_M))

    def first_finish(j, t):
        k = 2 * j + t
        slot = lax.rem(j, SLOTS) * 2 + t

        @pl.when(j >= SLOTS)
        def _():
            wait_bytes(s2buf.at[k - 2 * SLOTS], s2_send.at[k - 2 * SLOTS])
        wait_bytes(land.at[k], s1_recv.at[k])

        def body(b, carry):
            for i in range(TILES):
                cols = pl.ds(i * 128, 128)
                parts = [land[k, p * 8 + b, :, cols].astype(F32) for p in range(4)]
                acc1[slot, b, :, cols] = (parts[0] + parts[1]) + (parts[2] + parts[3])
            return carry
        lax.fori_loop(0, 8, body, 0)
        remote(acc1.at[slot, pl.ds((1 - b_of(t)) * 4, 4)], s2buf.at[k], s2_send.at[k], s2_recv.at[k], b_peer(t)).start()

    def second_finish(j, t):
        k = 2 * j + t
        slot = lax.rem(j, SLOTS) * 2 + t
        wait_bytes(s2buf.at[k], s2_recv.at[k])

        def body(zz, carry):
            for i in range(TILES):
                cols = pl.ds(i * 128, 128)
                s2buf[k, zz, :, cols] = s2buf[k, zz, :, cols] + acc1[slot, b_of(t) * 4 + zz, :, cols]
            return carry
        lax.fori_loop(0, 4, body, 0)
        for dz in range(1, 4):
            peer = lax.rem(z + dz, 4)
            remote(s2buf.at[k, peer], s3buf.at[k, dz - 1], s3_send.at[k], s3_recv.at[k], index_of(peer, y, x, c)).start()

    def third_finish(j, t):
        k = 2 * j + t
        wait_bytes(s3buf.at[k], s3_recv.at[k])
        total = n_acc[...]
        for i in range(TILES):
            cols = pl.ds(i * 128, 128)
            gs = ((s2buf[k, z, :, cols] + s3buf[k, 0, :, cols]) + (s3buf[k, 1, :, cols] + s3buf[k, 2, :, cols])) * (1.0 / GROUP)
            gsum[k, :, cols] = gs
            total = total + gs * gs
        n_acc[...] = total

    for j in range(AHEAD):
        for t in range(2):
            first_start(j, t)

    def small_start(i):
        remote(g_small.at[i], small_in.at[me], misc_send.at[0], misc_recv.at[0], i).start()
    all_to_all_small(me, small_start)
    small_in[me] = g_small[me]

    for i, ref in enumerate((nw, nm, nv)):
        wait_bytes(ref, load_sem.at[i])
    n_acc[...] = jnp.zeros_like(n_acc)
    rows_w[...] = jnp.zeros_like(rows_w)
    rows_u[...] = jnp.zeros_like(rows_u)

    def weight_squares(k, carry):
        total = rows_w[row_group(k)]
        for i in range(TILES):
            w = nw[k, :, pl.ds(i * 128, 128)]
            total = total + w * w
        rows_w[row_group(k)] = total
        return carry
    lax.fori_loop(0, CHUNKS, weight_squares, 0)

    def reduce_body(j, carry):
        @pl.when(j + AHEAD < PAIRS)
        def _():
            for t in range(2):
                first_start(j + AHEAD, t)

        @pl.when(j < PAIRS)
        def _():
            for t in range(2):
                first_finish(j, t)

        @pl.when(jnp.logical_and(j >= 1, j < PAIRS + 1))
        def _():
            for t in range(2):
                second_finish(j - 1, t)

        @pl.when(j >= 2)
        def _():
            for t in range(2):
                third_finish(j - 2, t)
        return carry
    lax.fori_loop(0, PAIRS + 2, reduce_body, 0)

    wait_bytes(small_in.at[pl.ds(0, GROUP - 1)], misc_recv.at[0])
    wait_bytes(small_in.at[pl.ds(0, GROUP - 1)], misc_send.at[0])
    gs_small = jnp.sum(small_in[...], axis=0) * (1.0 / GROUP)

    sub_iota = lax.broadcasted_iota(jnp.int32, (8, 128), 0)
    eye = lax.broadcasted_iota(jnp.int32, (96, 128), 0) == lax.broadcasted_iota(jnp.int32, (96, 128), 1)

    def to_row(column_parts):
        sums = jnp.sum(column_parts, axis=1, keepdims=True)
        return jnp.sum(jnp.where(eye, jnp.broadcast_to(sums, (96, 128)), 0.0), axis=0, keepdims=True)

    def message(row0, small, row3):
        half = jnp.sum(small, axis=0, keepdims=True)
        return (jnp.where(sub_iota == 0, jnp.broadcast_to(row0, (8, 128)), 0.0)
                + jnp.where(sub_iota == 1, jnp.broadcast_to(half[:, :128], (8, 128)), 0.0)
                + jnp.where(sub_iota == 2, jnp.broadcast_to(half[:, 128:], (8, 128)), 0.0)
                + jnp.where(sub_iota == 3, jnp.broadcast_to(row3, (8, 128)), 0.0))

    def sum_over_devices(value, slot, inbox):
        msg[slot] = value
        inbox[me] = value

        def start(i):
            remote(msg.at[slot], inbox.at[me], misc_send.at[1 + slot], misc_recv.at[1 + slot], i).start()
        all_to_all_small(me, start)
        wait_bytes(inbox.at[pl.ds(0, GROUP - 1)], misc_recv.at[1 + slot])
        wait_bytes(inbox.at[pl.ds(0, GROUP - 1)], misc_send.at[1 + slot])
        return jnp.sum(inbox[...], axis=0)

    small_w = w_small[...]
    small_sq = gs_small * gs_small
    square_row = jnp.sum(n_acc[...], axis=0, keepdims=True) + jnp.sum(small_sq[:, :128], axis=0, keepdims=True) + jnp.sum(small_sq[:, 128:], axis=0, keepdims=True)
    first_sums = sum_over_devices(message(to_row(rows_w[...].reshape(96, 128)), small_w * small_w, square_row), 0, inbox1)
    clip = jnp.minimum(1.0, MAX_NORM / jnp.sqrt(jnp.sum(first_sums[3:4], axis=1, keepdims=True)))
    clip_tile[...] = jnp.broadcast_to(clip, (ROWS, 128))

    def direction(k, carry):
        cl = clip_tile[...]
        total = rows_u[row_group(k)]
        for i in range(TILES):
            cols = pl.ds(i * 128, 128)
            u, m1, v1 = adam(gsum[k, :, cols], nw[k, :, cols], nm[k, :, cols], nv[k, :, cols], cl)
            nm[k, :, cols] = m1
            nv[k, :, cols] = v1
            gsum[k, :, cols] = u
            total = total + u * u
        rows_u[row_group(k)] = total
        return carry
    lax.fori_loop(0, CHUNKS, direction, 0)
    u_small, m1_small, v1_small = adam(gs_small, small_w, m_small[...], v_small[...], jnp.broadcast_to(clip, (8, 256)))
    nm_small[...] = m1_small
    nv_small[...] = v1_small
    second_sums = sum_over_devices(message(to_row(rows_u[...].reshape(96, 128)), u_small * u_small, jnp.zeros((1, 128), F32)), 1, inbox2)

    ratio_row = jnp.sqrt(first_sums[0:1]) / jnp.sqrt(second_sums[0:1])
    ratio_col = jnp.sum(jnp.where(eye, jnp.broadcast_to(ratio_row, (96, 128)), 0.0), axis=1, keepdims=True)
    ratio[...] = jnp.broadcast_to(LEARN_RATE * ratio_col, (96, 128)).reshape(6, ROWS, 128)

    lane = lax.broadcasted_iota(jnp.int32, (1, 128), 1)

    def small_totals(sums):
        upper = sums[2:3]
        wide = jnp.where(lane >= 64, upper, 0.0)
        for shift in (64, 32, 16):
            wide = wide + pltpu.roll(wide, shift, 1)
        return sums[1:2], jnp.where(lane >= 64, wide, upper)

    w_low, w_high = small_totals(first_sums)
    u_low, u_high = small_totals(second_sums)
    r_low = LEARN_RATE * (jnp.sqrt(w_low) / jnp.sqrt(u_low))
    r_high = LEARN_RATE * (jnp.sqrt(w_high) / jnp.sqrt(u_high))
    r_small = jnp.concatenate([jnp.broadcast_to(r_low, (8, 128)), jnp.broadcast_to(r_high, (8, 128))], axis=1)
    new_small = small_w - r_small * u_small
    nw_small[...] = new_small
    small_u[...] = new_small
    small_all[me] = new_small

    def small_gather(i):
        remote(small_u, small_all.at[me], misc_send.at[3], misc_recv.at[3], i).start()
    all_to_all_small(me, small_gather)

    def gather_z(j, t):
        k = 2 * j + t
        mine = a_of(t) * 16 + c * 8 + b_of(t) * 4 + z
        rr = ratio[row_group(k)]
        for i in range(TILES):
            cols = pl.ds(i * 128, 128)
            w1 = nw[k, :, cols] - rr * gsum[k, :, cols]
            nw[k, :, cols] = w1
            land[k, mine, :, cols] = w1.astype(BF16)
        for dz in range(1, 4):
            remote(land.at[k, mine], land.at[k, mine], s3_send.at[k], s3_recv.at[k], index_of(lax.rem(z + dz, 4), y, x, c)).start()

    def gather_b(j, t):
        k = 2 * j + t
        wait_bytes(land.at[k, pl.ds(0, 3)], s3_recv.at[k])
        part = land.at[k, pl.ds(a_of(t) * 16 + c * 8 + b_of(t) * 4, 4)]
        remote(part, part, s2_send.at[k], s2_recv.at[k], b_peer(t)).start()

    def gather_a(j, t):
        k = 2 * j + t
        wait_bytes(land.at[k, pl.ds(0, 4)], s2_recv.at[k])
        part = land.at[k, pl.ds(a_of(t) * 16 + c * 8, 8)]
        remote(part, part, s1_send.at[k], s1_recv.at[k], a_peer(t, 1, 0)).start()
        remote(part, part, d_send.at[k], d_recv.at[k], a_peer(t, 0, 1)).start()

    def gather_core(j, t):
        k = 2 * j + t
        wait_bytes(land.at[k, pl.ds(0, 8)], s1_recv.at[k])
        part = land.at[k, pl.ds((1 - a_of(t)) * 16 + c * 8, 8)]
        remote(part, part, d_send.at[k], d_recv.at[k], a_peer(t, 0, 1)).start()

    def gather_body(j, carry):
        @pl.when(j < PAIRS)
        def _():
            for t in range(2):
                gather_z(j, t)

        @pl.when(jnp.logical_and(j >= 1, j < PAIRS + 1))
        def _():
            for t in range(2):
                gather_b(j - 1, t)

        @pl.when(jnp.logical_and(j >= 2, j < PAIRS + 2))
        def _():
            for t in range(2):
                gather_a(j - 2, t)

        @pl.when(j >= 3)
        def _():
            for t in range(2):
                gather_core(j - 3, t)
        return carry

    def drain_reduce(k, carry):
        wait_bytes(land.at[k, pl.ds(0, 24)], s1_send.at[k])

        @pl.when(k >= CHUNKS - 2 * SLOTS)
        def _():
            wait_bytes(s2buf.at[k], s2_send.at[k])
        wait_bytes(s3buf.at[k], s3_send.at[k])
        return carry
    lax.fori_loop(0, CHUNKS, drain_reduce, 0)
    lax.fori_loop(0, PAIRS + 3, gather_body, 0)

    def drain_gather(k, carry):
        wait_bytes(land.at[k, pl.ds(0, 16)], d_recv.at[k])
        wait_bytes(land.at[k, pl.ds(0, 16)], d_send.at[k])
        wait_bytes(land.at[k, pl.ds(0, 8)], s1_send.at[k])
        wait_bytes(land.at[k, pl.ds(0, 4)], s2_send.at[k])
        wait_bytes(land.at[k, pl.ds(0, 3)], s3_send.at[k])
        return carry
    lax.fori_loop(0, CHUNKS, drain_gather, 0)
    wait_bytes(small_all.at[pl.ds(0, GROUP - 1)], misc_recv.at[3])
    wait_bytes(small_all.at[pl.ds(0, GROUP - 1)], misc_send.at[3])


def store_kernel(land, nw, nm, nv, rep_attn, rep_mlp, w_attn, w_mlp, m_attn, m_mlp, v_attn, v_mlp, sem):
    state_out = ((nw, w_attn, w_mlp), (nm, m_attn, m_mlp), (nv, v_attn, v_mlp))

    def pair_body(j, carry):
        for t in range(2):
            k = 2 * j + t

            def issue(rep, which, own, rg, sub):
                def body(q, carry):
                    aa, cc, bb, zz = q // 16, lax.rem(q // 8, 2), lax.rem(q // 4, 2), lax.rem(q, 4)
                    owner = index_of(zz, bb, aa, cc) if t == 0 else index_of(zz, aa, bb, cc)
                    pltpu.make_async_copy(land.at[k, q], rep.at[pl.ds(rg * ROWS, ROWS), pl.ds(pl.multiple_of(owner * own + sub * WIDTH, 128), WIDTH)], sem.at[0]).start()
                    return carry
                lax.fori_loop(0, 32, body, 0, unroll=4)
                for i, refs in enumerate(state_out):
                    pltpu.make_async_copy(refs[0].at[k], refs[1 + which].at[pl.ds(rg * ROWS, ROWS), pl.ds(pl.multiple_of(sub * WIDTH, 128), WIDTH)], sem.at[1 + i]).start()
            bank_of(k, lambda rg, sub: issue(rep_attn, 0, OWN_A, rg, sub), lambda rg, sub: issue(rep_mlp, 1, OWN_M, rg, sub))
        return carry
    lax.fori_loop(0, PAIRS, pair_body, 0)
    wait_bytes(land, sem.at[0])
    for i, refs in enumerate(state_out):
        wait_bytes(refs[0], sem.at[1 + i])


def pack_small(vec, wide, fill):
    lead = vec.shape[:-2]
    vec_t = jnp.swapaxes(vec, -1, -2)
    wide_t = jnp.moveaxis(wide.reshape(lead + (16, 4, 8)), (-3, -2, -1), (-1, -2, -3)).reshape(lead + (8, 64))
    pad = jnp.full(lead + (8, 46), fill, vec.dtype)
    return jnp.concatenate([vec_t, pad, wide_t], axis=-1)


def unpack_small(packed):
    lead = packed.shape[:-2]
    vec = jnp.swapaxes(packed[..., :146], -1, -2)
    wide = jnp.moveaxis(packed[..., 192:].reshape(lead + (8, 4, 16)), (-3, -2, -1), (-1, -2, -3)).reshape(lead + (16, 32))
    return vec, wide


def solution(mesh):
    grad_spec = P(AXIS, None, None)
    shard_spec = P(None, AXIS)
    full_spec = P(None, None)

    def local_step(g_attn, g_mlp, g_wide, g_vec, w_attn, w_mlp, w_wide, w_vec, m_attn, m_mlp, m_wide, m_vec, v_attn, v_mlp, v_wide, v_vec):
        g_small = pack_small(jnp.moveaxis(g_vec.reshape(146, GROUP, 8), 1, 0), jnp.moveaxis(g_wide.reshape(16, GROUP, 32), 1, 0), 0.0).astype(F32)
        w_small = pack_small(w_vec, w_wide, 1.0)
        m_small = pack_small(m_vec, m_wide, 0.0)
        v_small = pack_small(v_vec, v_wide, 1.0)
        hbm = pl.BlockSpec(memory_space=pl.ANY)
        vmem = pl.BlockSpec(memory_space=pltpu.VMEM)
        block = (CHUNKS, ROWS, WIDTH)
        small = jax.ShapeDtypeStruct((8, 256), F32)
        dma = pltpu.SemaphoreType.DMA
        land, nw, nm, nv, small_all, nw_small, nm_small, nv_small = pl.pallas_call(
            step_kernel,
            out_shape=(pltpu.VMEM((CHUNKS, 32, ROWS, WIDTH), BF16), pltpu.VMEM(block, F32), pltpu.VMEM(block, F32), pltpu.VMEM(block, F32),
                       pltpu.VMEM((GROUP, 8, 256), F32), small, small, small),
            in_specs=[hbm, hbm, vmem] + [hbm] * 6 + [vmem] * 3,
            out_specs=(vmem,) * 8,
            scratch_shapes=[
                pltpu.VMEM((2 * SLOTS, 8, ROWS, WIDTH), F32),
                pltpu.VMEM((CHUNKS, 4, ROWS, WIDTH), F32),
                pltpu.VMEM((CHUNKS, 3, ROWS, WIDTH), F32),
                pltpu.VMEM(block, F32),
                pltpu.VMEM((GROUP, 8, 256), F32),
                pltpu.VMEM((8, 256), F32),
                pltpu.VMEM((2, 8, 128), F32),
                pltpu.VMEM((GROUP, 8, 128), F32),
                pltpu.VMEM((GROUP, 8, 128), F32),
                pltpu.VMEM((6, ROWS, 128), F32),
                pltpu.VMEM((6, ROWS, 128), F32),
                pltpu.VMEM((6, ROWS, 128), F32),
                pltpu.VMEM((ROWS, 128), F32),
                pltpu.VMEM((ROWS, 128), F32),
                dma((CHUNKS,)), dma((CHUNKS,)), dma((CHUNKS,)), dma((CHUNKS,)), dma((CHUNKS,)), dma((CHUNKS,)), dma((CHUNKS,)), dma((CHUNKS,)),
                dma((3,)), dma((4,)), dma((4,)),
            ],
            compiler_params=pltpu.CompilerParams(collective_id=0, has_side_effects=True, vmem_limit_bytes=26 * 1024 * 1024),
            name="lamb_step",
        )(g_attn, g_mlp, g_small, w_attn, w_mlp, m_attn, m_mlp, v_attn, v_mlp, w_small, m_small, v_small)
        shard_a = jax.ShapeDtypeStruct((64, OWN_A), F32)
        shard_m = jax.ShapeDtypeStruct((32, OWN_M), F32)
        rep_attn, rep_mlp, nw_attn, nw_mlp, nm_attn, nm_mlp, nv_attn, nv_mlp = pl.pallas_call(
            store_kernel,
            out_shape=(jax.ShapeDtypeStruct((64, OWN_A * GROUP), BF16), jax.ShapeDtypeStruct((32, OWN_M * GROUP), BF16),
                       shard_a, shard_m, shard_a, shard_m, shard_a, shard_m),
            in_specs=[vmem] * 4,
            out_specs=(hbm,) * 8,
            scratch_shapes=[dma((4,))],
            compiler_params=pltpu.CompilerParams(vmem_limit_bytes=4 * 1024 * 1024),
            name="store_results",
        )(land, nw, nm, nv)
        rep_vec, rep_wide = unpack_small(small_all.astype(BF16))
        rep_vec = jnp.moveaxis(rep_vec, 0, 1).reshape(146, 256)
        rep_wide = jnp.moveaxis(rep_wide, 0, 1).reshape(16, 1024)
        nw_vec, nw_wide = unpack_small(nw_small)
        nm_vec, nm_wide = unpack_small(nm_small)
        nv_vec, nv_wide = unpack_small(nv_small)
        return (rep_attn, rep_mlp, rep_wide, rep_vec, nw_attn, nw_mlp, nw_wide, nw_vec, nm_attn, nm_mlp, nm_wide, nm_vec, nv_attn, nv_mlp, nv_wide, nv_vec)

    return jax.shard_map(local_step, mesh=mesh, in_specs=(grad_spec,) * 4 + (shard_spec,) * 12, out_specs=(full_spec,) * 4 + (shard_spec,) * 12, check_vma=False)
```

time: 931 us -> 424 us (0.46)
  waiting for transfers between devices: 596 us -> 0 us
  Pallas kernels: 0 us -> 390 us
  blocking collectives: 175 us -> 0 us
  local copies, waits for them, and re-layouts: 86.8 us -> 27.2 us
  starting transfers between devices: 28.3 us -> 0 us
  other arithmetic: 27.1 us -> 3.57 us
  between operations: 17.6 us -> 0.77 us
    all_to_all x4 -> x0, waiting for transfers between devices: 485 us -> none  [local_step(): received = lax.all_to_all(by_owner, 'data', 1, 1, tiled=True)]
    pallas_call x0 -> x2, Pallas kernels: none -> 390 us  [the longest x1 374 us: local_step(): pl.pallas_call(step_kernel, out_shape=(pltpu.VMEM((CHUNKS, 32, ROWS, WIDT...]
    all_gather x2 -> x0, waiting for transfers between devices: 110 us -> none  [local_step(): lax.all_gather(new_weight.astype(jnp.bfloat16), 'data', axis=1, tiled=True)]
    psum x2 -> x0, blocking collectives: 96.6 us -> none  [the longest x1 54.4 us: local_step(): lax.psum(local_square, 'data')]
    all_gather x2 -> x0, blocking collectives: 77.9 us -> none  [local_step(): lax.all_gather(new_weight.astype(jnp.bfloat16), 'data', axis=1, tiled=True)]
    reshape x4 -> x13, local copies, waits for them, and re-layouts: 34.4 us -> 2.35 us  [the longest x1 0.92 us: local_step(): g_wide.reshape(16, GROUP, 32)]
    unnamed x37 -> x18, local copies, waits for them, and re-layouts: 52.2 us -> 22.5 us
    all_to_all x4 -> x0, starting transfers between devices: 28 us -> none  [local_step(): received = lax.all_to_all(by_owner, 'data', 1, 1, tiled=True)]
  transfers between devices with their start and end apart: 6 -> 0, of which waited for: 4 -> 0; matrix products, arithmetic and copies ran while one was open for 8% -> 0% of each run, Pallas kernels for 0% -> 0%
where the time goes in v1:
time: 424 us; the launch traced here: 421 us
  Pallas kernels  390 us (92%)
  local copies, waits for them, and re-layouts  27.2 us (6%)
    pallas_call x1, Pallas kernels, local_step(): pl.pallas_call(step_kernel, out_shape=(pltpu.VMEM((CHUNKS, 32, ROWS, WIDT...  374 us
    unnamed x18, local copies, waits for them, and re-layouts  22.5 us
    pallas_call x1, Pallas kernels, local_step(): pl.pallas_call(store_kernel, out_shape=(jax.ShapeDtypeStruct((64, OWN_A *...  16 us

profile of v1, /device:TPU:0, one launch (start us, length us, event | category | flops | bytes accessed | tf_op | source)
XLA Modules:
  0.0 421.5 jit_solution(556851954612556211)
XLA Ops:
  0.7 0.1 pad.10.clone
  0.7 0.1 pad.7.clone
  0.8 0.1 pad.4.clone
  0.9 0.8 copy.62
  1.7 0.1 reshape.97
  1.8 0.8 copy.64
  2.5 0.1 reshape.99
  2.6 1.4 pad_maximum_fusion.1.m_small
  4.0 0.8 copy.66
  4.8 0.1 reshape.101
  4.8 1.4 pad_maximum_fusion.2
  6.2 0.9 reshape.93
  7.2 0.1 copy.59
  7.3 0.1 copy.60
  7.4 0.1 copy.61
  7.5 1.0 copy.58
  8.5 0.8 maximum_convert_fusion.g_small
  9.3 373.9 %lamb_step.1 = (bf16[24,32,16,1024]{3,2,1,0:T(8,128)(2,1)S(1)}, f32[24,16,1024]{2,1,0:T(8,128)S(1)}, f32[24,16,1024]{2,1,0:T(8,128)S(1)}, f32[24,16,1024]{2,1,0:...) custom-call(bf16[1,64,65536]{2,1,0:T(8,128)(2,1)} %g_attn.1, ...), custom_call_target="tpu_custom_call" | custom-call | tf_op jit(solution)/shard_map/lamb_step/pallas_call | solution.py:445
  383.2 0.0 copy-start
  383.2 8.3 %copy-done = bf16[24,32,16,1024]{3,2,1,0:T(8,128)(2,1)} copy-done((bf16[24,32,16,1024]{3,2,1,0:T(8,128)(2,1)}, bf16[24,32,16,1024]{3,2,1,0:T(8,128)(2,1)S(1)}, u32[]{:S(2)}) %copy-start) | copy-done | bytes 25165848
  391.5 0.0 copy-start.1
  391.5 8.2 %copy-done.1 = bf16[24,32,16,1024]{3,2,1,0:T(8,128)(2,1)S(1)} copy-done((bf16[24,32,16,1024]{3,2,1,0:T(8,128)(2,1)S(1)}, bf16[24,32,16,1024]{3,2,1,0:T(8,128)(2,1)}, u32[]{:S(2)}) %copy-start.1) | copy-done | bytes 25165848
  399.7 0.0 copy-start.2
  399.7 0.0 copy-start.3
  399.7 0.0 copy-start.4
  399.7 16.0 %store_results.1 = (bf16[64,65536]{1,0:T(8,128)(2,1)}, bf16[32,262144]{1,0:T(8,128)(2,1)}, f32[64,2048]{1,0:T(8,128)}, f32[32,8192]{1,0:T(8,128)}, f32[64,2048]{...) custom-call(bf16[24,32,16,1024]{3,2,1,0:T(8,128)(2,1)S(1)} %copy-done.1, ...), custom_call_target="tpu_custom_call" | custom-call | tf_op jit(solution)/shard_map/store_results/pallas_call | solution.py:474
  415.7 0.0 copy-done.2
  415.8 0.1 slice.26
  415.8 0.6 slice_bitcast_fusion.3
  416.4 0.0 copy-done.3
  416.4 0.1 slice.28
  416.5 0.0 copy-done.4
  416.5 0.1 slice.30
  416.6 0.6 slice_bitcast_fusion.1
  417.2 0.1 reshape.110
  417.3 0.7 copy.77
  417.9 0.1 reshape.108
  418.0 0.7 copy.76
  418.7 0.1 reshape.106
  418.8 0.7 copy.75
  419.5 0.1 slice.32
  419.6 0.7 copy.74
  420.3 0.1 copy.68
  420.5 0.1 copy.82
  420.6 0.1 copy.70
  420.7 0.8 reshape.104
  (11 shorter events, 0.1 us)
Async XLA Ops:
  383.2 8.3 %copy-start = (bf16[24,32,16,1024]{3,2,1,0:T(8,128)(2,1)}, bf16[24,32,16,1024]{3,2,1,0:T(8,128)(2,1)S(1)}, u32[]{:S(2)}) copy-start(bf16[24,32,16,1024]{3,2,1,0:T(8,128)(2,1)S(1)} %get-tuple-element.32.land) | copy-start | bytes 75497472
  391.5 8.2 %copy-start.1 = (bf16[24,32,16,1024]{3,2,1,0:T(8,128)(2,1)S(1)}, bf16[24,32,16,1024]{3,2,1,0:T(8,128)(2,1)}, u32[]{:S(2)}) copy-start(bf16[24,32,16,1024]{3,2,1,0:T(8,128)(2,1)} %copy-done) | copy-start | bytes 75497472
  399.7 16.1 %copy-start.2 = (f32[8,256]{1,0:T(8,128)S(1)}, f32[8,256]{1,0:T(8,128)}, u32[]{:S(2)}) copy-start(f32[8,256]{1,0:T(8,128)} %get-tuple-element.41) | copy-start | bytes 24580
  399.7 16.7 %copy-start.3 = (f32[8,256]{1,0:T(8,128)S(1)}, f32[8,256]{1,0:T(8,128)}, u32[]{:S(2)}) copy-start(f32[8,256]{1,0:T(8,128)} %get-tuple-element.44) | copy-start | bytes 24580
  399.7 16.8 %copy-start.4 = (f32[8,256]{1,0:T(8,128)S(1)}, f32[8,256]{1,0:T(8,128)}, u32[]{:S(2)}) copy-start(f32[8,256]{1,0:T(8,128)} %get-tuple-element.47) | copy-start | bytes 24580

commit v2 on v1

v2 whole, which is shorter than its diff:
```python
import jax
import jax.numpy as jnp
from jax import lax
from jax.experimental import pallas as pl
from jax.experimental.pallas import tpu as pltpu
from jax.sharding import PartitionSpec as P

STEP_NUMBER = 10
LEARN_RATE = 0.04
BETA_FIRST = 0.9
BETA_SECOND = 0.999
EPSILON = 1e-6
WEIGHT_DECAY = 0.01
MAX_NORM = 1.0

GROUP = 32
AXIS = "data"
MESH = pl.DeviceIdType.MESH
F32 = jnp.float32
BF16 = jnp.bfloat16

ROWS = 16
WIDTH = 1024
OWN_A = 2048
OWN_M = 8192
SUB_A = OWN_A // WIDTH
SUB_M = OWN_M // WIDTH
CHUNKS_A = 4 * SUB_A
CHUNKS_M = 2 * SUB_M
CHUNKS = CHUNKS_A + CHUNKS_M
PAIRS = CHUNKS // 2
AHEAD = 2
SLOTS = 3
TILES = WIDTH // 128


def coords():
    me = lax.axis_index(AXIS)
    return me // 8, lax.rem(me // 4, 2), lax.rem(me // 2, 2), lax.rem(me, 2)


def index_of(z, y, x, c):
    return ((z * 2 + y) * 2 + x) * 2 + c


def remote(src, dst, send_sem, recv_sem, device):
    return pltpu.make_async_remote_copy(src_ref=src, dst_ref=dst, send_sem=send_sem, recv_sem=recv_sem, device_id=(device,), device_id_type=MESH)


def wait_bytes(ref, sem):
    pltpu.make_async_copy(ref, ref, sem).wait()


def bank_of(k, attn_case, mlp_case):
    @pl.when(k < CHUNKS_A)
    def _():
        attn_case(k // SUB_A, lax.rem(k, SUB_A))

    @pl.when(k >= CHUNKS_A)
    def _():
        local = k - CHUNKS_A
        mlp_case(local // SUB_M, lax.rem(local, SUB_M))


def row_group(k):
    return jnp.where(k < CHUNKS_A, k // SUB_A, 4 + (k - CHUNKS_A) // SUB_M)


def adam(gs, w, m, v, clip):
    clipped = clip * gs
    new_m = BETA_FIRST * m + (1.0 - BETA_FIRST) * clipped
    new_v = BETA_SECOND * v + (1.0 - BETA_SECOND) * (clipped * clipped)
    u = (new_m * (1.0 / (1.0 - BETA_FIRST ** STEP_NUMBER))) / (jnp.sqrt(new_v * (1.0 / (1.0 - BETA_SECOND ** STEP_NUMBER))) + EPSILON) + WEIGHT_DECAY * w
    return u, new_m, new_v


def to_others(me, start_one):
    def body(i, carry):
        start_one(lax.rem(me + 1 + i, GROUP))
        return carry
    lax.fori_loop(0, GROUP - 1, body, 0)


def flip(bit, other):
    return bit + other - 2 * bit * other


def pack_state(vec_ref, wide_ref, flat, square, fill):
    flat[...] = jnp.zeros_like(flat)
    flat[0:8, 0:146] = vec_ref[...]
    square[...] = jnp.zeros_like(square)
    square[0:16, 0:32] = wide_ref[...]
    vec = flat[...]
    wide_t = square[...].T
    wide = pltpu.roll(wide_t[0:8], 64, 1)
    for g in range(1, 4):
        wide = wide + pltpu.roll(wide_t[8 * g:8 * g + 8], 64 + 16 * g, 1)
    lane = lax.broadcasted_iota(jnp.int32, (8, 256), 1)
    packed = jnp.concatenate([vec[:, :128], vec[:, 128:] + wide], axis=1)
    return jnp.where(jnp.logical_and(lane >= 146, lane < 192), fill, packed)


def unpack_state(packed, vec_ref, wide_ref, square):
    vec_ref[...] = packed[:, 0:146]
    square[...] = jnp.zeros_like(square)
    for g in range(4):
        square[8 * g:8 * g + 8, :] = pltpu.roll(packed[:, 128:], (64 - 16 * g) % 128, 1)
    wide_ref[...] = square[...].T[0:16, 0:32]


def pack_grads(g_vec, g_wide, g_small, big, long):
    big[...] = jnp.zeros_like(big)
    big[0:146, :] = g_vec[0].astype(F32)
    long[...] = jnp.zeros_like(long)
    long[0:16, :] = g_wide[0].astype(F32)
    vec = big[...].T
    wide_t = long[...].T.reshape(GROUP, 4, 8, 128)
    wide = pltpu.roll(wide_t[:, 0].reshape(GROUP * 8, 128), 64, 1)
    for g in range(1, 4):
        wide = wide + pltpu.roll(wide_t[:, g].reshape(GROUP * 8, 128), 64 + 16 * g, 1)
    g_small[:, :, 0:128] = vec[:, :128].reshape(GROUP, 8, 128)
    g_small[:, :, 128:256] = (vec[:, 128:] + wide).reshape(GROUP, 8, 128)


def unpack_replica(small_all, rep_vec, rep_wide):
    rep_vec[...] = small_all[...].reshape(GROUP * 8, 256).T[0:146].astype(BF16)
    upper = small_all[:, :, 128:256].reshape(GROUP * 8, 128)
    parts = [pltpu.roll(upper, (64 - 16 * g) % 128, 1).reshape(GROUP, 1, 8, 128) for g in range(4)]
    rep_wide[...] = jnp.concatenate(parts, axis=1).reshape(GROUP * 32, 128).T[0:16].astype(BF16)


def step_kernel(g_attn, g_mlp, g_vec, g_wide, w_attn, w_mlp, m_attn, m_mlp, v_attn, v_mlp, w_vec, w_wide, m_vec, m_wide, v_vec, v_wide,
                land, nw, nm, nv, rep_vec, rep_wide, nw_vec, nw_wide, nm_vec, nm_wide, nv_vec, nv_wide,
                acc1, s2buf, s3buf, s4buf, gsum, g_small, small_in, small_all, small_new, state_small, big, long, flat, square,
                msg, inbox1, inbox2, rows_w, rows_u, ratio, clip_tile, n_acc,
                s1_send, s1_recv, s2_send, s2_recv, s3_send, s3_recv, s4_send, s4_recv, d_send, d_recv, load_sem, misc_send, misc_recv):
    me = lax.axis_index(AXIS)
    z, y, x, c = coords()
    zh, zl = z // 2, lax.rem(z, 2)

    barrier = pltpu.get_barrier_semaphore()
    to_others(me, lambda i: pl.semaphore_signal(barrier, inc=1, device_id=(i,), device_id_type=MESH))

    def load_state(k, carry):
        def issue(which, rg, sub):
            for i, refs in enumerate(((w_attn, w_mlp, nw), (m_attn, m_mlp, nm), (v_attn, v_mlp, nv))):
                pltpu.make_async_copy(refs[which].at[pl.ds(rg * ROWS, ROWS), pl.ds(pl.multiple_of(sub * WIDTH, 128), WIDTH)], refs[2].at[k], load_sem.at[i]).start()
        bank_of(k, lambda rg, sub: issue(0, rg, sub), lambda rg, sub: issue(1, rg, sub))
        return carry
    lax.fori_loop(0, CHUNKS, load_state, 0)
    pack_grads(g_vec, g_wide, g_small, big, long)

    pl.semaphore_wait(barrier, GROUP - 1)

    def a_of(t):
        return x if t == 0 else y

    def b_of(t):
        return y if t == 0 else x

    def a_peer(t, da, dc):
        cc = flip(c, dc)
        return index_of(z, y, flip(x, da), cc) if t == 0 else index_of(z, flip(y, da), x, cc)

    def b_peer(t):
        return index_of(z, 1 - y, x, c) if t == 0 else index_of(z, y, 1 - x, c)

    low_peer = index_of(zh * 2 + 1 - zl, y, x, c)
    high_peer = index_of((1 - zh) * 2 + zl, y, x, c)

    def first_start(j, t):
        k = 2 * j + t

        def issue(grad, rg, sub, own):
            def body(b, carry):
                zz = lax.rem(b, 2) * 2 + b // 4
                bb = lax.rem(b // 2, 2)
                for da in range(2):
                    for dc in range(2):
                        aa, cc = flip(a_of(t), da), flip(c, dc)
                        owner = index_of(zz, bb, aa, cc) if t == 0 else index_of(zz, aa, bb, cc)
                        src = grad.at[0, pl.ds(rg * ROWS, ROWS), pl.ds(pl.multiple_of(owner * own + sub * WIDTH, 128), WIDTH)]
                        dst = land.at[k, (da * 2 + dc) * 8 + b]
                        if da == 0 and dc == 0:
                            pltpu.make_async_copy(src, dst, s1_recv.at[k]).start()
                        else:
                            remote(src, dst, s1_send.at[k], s1_recv.at[k], a_peer(t, da, dc)).start()
                return carry
            lax.fori_loop(0, 8, body, 0)
        bank_of(k, lambda rg, sub: issue(g_attn, rg, sub, OWN_A), lambda rg, sub: issue(g_mlp, rg, sub, OWN_M))

    def first_finish(j, t):
        k = 2 * j + t
        slot = lax.rem(j, SLOTS) * 2 + t

        @pl.when(j >= SLOTS)
        def _():
            wait_bytes(s2buf.at[k - 2 * SLOTS], s2_send.at[k - 2 * SLOTS])
        wait_bytes(land.at[k], s1_recv.at[k])

        def body(b, carry):
            for i in range(TILES):
                cols = pl.ds(i * 128, 128)
                parts = [land[k, p * 8 + b, :, cols].astype(F32) for p in range(4)]
                acc1[slot, b, :, cols] = (parts[0] + parts[1]) + (parts[2] + parts[3])
            return carry
        lax.fori_loop(0, 8, body, 0)
        remote(acc1.at[slot, pl.ds((1 - zl) * 4, 4)], s2buf.at[k], s2_send.at[k], s2_recv.at[k], low_peer).start()

    def second_finish(j, t):
        k = 2 * j + t
        slot = lax.rem(j, SLOTS) * 2 + t
        wait_bytes(s2buf.at[k], s2_recv.at[k])

        def body(b, carry):
            for i in range(TILES):
                cols = pl.ds(i * 128, 128)
                s2buf[k, b, :, cols] = s2buf[k, b, :, cols] + acc1[slot, zl * 4 + b, :, cols]
            return carry
        lax.fori_loop(0, 4, body, 0)
        remote(s2buf.at[k, pl.ds((1 - b_of(t)) * 2, 2)], s3buf.at[k], s3_send.at[k], s3_recv.at[k], b_peer(t)).start()

    def third_finish(j, t):
        k = 2 * j + t
        wait_bytes(s3buf.at[k], s3_recv.at[k])
        for b in range(2):
            for i in range(TILES):
                cols = pl.ds(i * 128, 128)
                s3buf[k, b, :, cols] = s3buf[k, b, :, cols] + s2buf[k, b_of(t) * 2 + b, :, cols]
        remote(s3buf.at[k, 1 - zh], s4buf.at[k], s4_send.at[k], s4_recv.at[k], high_peer).start()

    def fourth_finish(j, t):
        k = 2 * j + t
        wait_bytes(s4buf.at[k], s4_recv.at[k])
        total = n_acc[...]
        for i in range(TILES):
            cols = pl.ds(i * 128, 128)
            gs = (s3buf[k, zh, :, cols] + s4buf[k, :, cols]) * (1.0 / GROUP)
            gsum[k, :, cols] = gs
            total = total + gs * gs
        n_acc[...] = total

    for j in range(AHEAD):
        for t in range(2):
            first_start(j, t)

    def small_start(i):
        remote(g_small.at[i], small_in.at[me], misc_send.at[0], misc_recv.at[0], i).start()
    to_others(me, small_start)
    small_in[me] = g_small[me]

    for i, (vec_ref, wide_ref, fill) in enumerate(((w_vec, w_wide, 1.0), (m_vec, m_wide, 0.0), (v_vec, v_wide, 1.0))):
        state_small[i] = pack_state(vec_ref, wide_ref, flat, square, fill)
    for i, ref in enumerate((nw, nm, nv)):
        wait_bytes(ref, load_sem.at[i])
    n_acc[...] = jnp.zeros_like(n_acc)
    rows_w[...] = jnp.zeros_like(rows_w)
    rows_u[...] = jnp.zeros_like(rows_u)

    def weight_squares(k, carry):
        total = rows_w[row_group(k)]
        for i in range(TILES):
            w = nw[k, :, pl.ds(i * 128, 128)]
            total = total + w * w
        rows_w[row_group(k)] = total
        return carry
    lax.fori_loop(0, CHUNKS, weight_squares, 0)

    def pipeline(stages, first=None):
        def body(j, carry):
            if first is not None:
                @pl.when(j + AHEAD < PAIRS)
                def _():
                    for t in range(2):
                        first(j + AHEAD, t)
            for lag, stage in enumerate(stages):
                @pl.when(jnp.logical_and(j >= lag, j < PAIRS + lag))
                def _():
                    for t in range(2):
                        stage(j - lag, t)
            return carry
        lax.fori_loop(0, PAIRS + len(stages) - 1, body, 0)
    pipeline((first_finish, second_finish, third_finish, fourth_finish), first_start)

    wait_bytes(small_in.at[pl.ds(0, GROUP - 1)], misc_recv.at[0])
    wait_bytes(small_in.at[pl.ds(0, GROUP - 1)], misc_send.at[0])
    gs_small = jnp.sum(small_in[...], axis=0) * (1.0 / GROUP)

    sub_iota = lax.broadcasted_iota(jnp.int32, (4, 128), 0)
    eye = lax.broadcasted_iota(jnp.int32, (96, 128), 0) == lax.broadcasted_iota(jnp.int32, (96, 128), 1)

    def to_row(column_parts):
        sums = jnp.sum(column_parts, axis=1, keepdims=True)
        return jnp.sum(jnp.where(eye, jnp.broadcast_to(sums, (96, 128)), 0.0), axis=0, keepdims=True)

    def message(row0, small, row3):
        half = jnp.sum(small, axis=0, keepdims=True)
        return (jnp.where(sub_iota == 0, jnp.broadcast_to(row0, (4, 128)), 0.0)
                + jnp.where(sub_iota == 1, jnp.broadcast_to(half[:, :128], (4, 128)), 0.0)
                + jnp.where(sub_iota == 2, jnp.broadcast_to(half[:, 128:], (4, 128)), 0.0)
                + jnp.where(sub_iota == 3, jnp.broadcast_to(row3, (4, 128)), 0.0))

    def sum_over_devices(value, slot, inbox):
        msg[slot] = value
        inbox[me] = value

        def start(i):
            remote(msg.at[slot], inbox.at[me], misc_send.at[1 + slot], misc_recv.at[1 + slot], i).start()
        to_others(me, start)
        wait_bytes(inbox.at[pl.ds(0, GROUP - 1)], misc_recv.at[1 + slot])
        wait_bytes(inbox.at[pl.ds(0, GROUP - 1)], misc_send.at[1 + slot])
        return jnp.sum(inbox[...], axis=0)

    small_w = state_small[0]
    small_sq = gs_small * gs_small
    square_row = jnp.sum(n_acc[...], axis=0, keepdims=True) + jnp.sum(small_sq[:, :128], axis=0, keepdims=True) + jnp.sum(small_sq[:, 128:], axis=0, keepdims=True)
    first_sums = sum_over_devices(message(to_row(rows_w[...].reshape(96, 128)), small_w * small_w, square_row), 0, inbox1)
    clip = jnp.minimum(1.0, MAX_NORM / jnp.sqrt(jnp.sum(first_sums[3:4], axis=1, keepdims=True)))
    clip_tile[...] = jnp.broadcast_to(clip, (ROWS, 128))

    def direction(k, carry):
        cl = clip_tile[...]
        total = rows_u[row_group(k)]
        for i in range(TILES):
            cols = pl.ds(i * 128, 128)
            u, m1, v1 = adam(gsum[k, :, cols], nw[k, :, cols], nm[k, :, cols], nv[k, :, cols], cl)
            nm[k, :, cols] = m1
            nv[k, :, cols] = v1
            gsum[k, :, cols] = u
            total = total + u * u
        rows_u[row_group(k)] = total
        return carry
    lax.fori_loop(0, CHUNKS, direction, 0)
    u_small, m1_small, v1_small = adam(gs_small, small_w, state_small[1], state_small[2], jnp.broadcast_to(clip, (8, 256)))
    second_sums = sum_over_devices(message(to_row(rows_u[...].reshape(96, 128)), u_small * u_small, jnp.zeros((1, 128), F32)), 1, inbox2)

    ratio_row = jnp.sqrt(first_sums[0:1]) / jnp.sqrt(second_sums[0:1])
    ratio_col = jnp.sum(jnp.where(eye, jnp.broadcast_to(ratio_row, (96, 128)), 0.0), axis=1, keepdims=True)
    ratio[...] = jnp.broadcast_to(LEARN_RATE * ratio_col, (96, 128)).reshape(6, ROWS, 128)

    lane = lax.broadcasted_iota(jnp.int32, (1, 128), 1)

    def small_totals(sums):
        upper = sums[2:3]
        wide = jnp.where(lane >= 64, upper, 0.0)
        for shift in (64, 32, 16):
            wide = wide + pltpu.roll(wide, shift, 1)
        return sums[1:2], jnp.where(lane >= 64, wide, upper)

    def gather_high(j, t):
        k = 2 * j + t
        mine = a_of(t) * 16 + c * 8 + zl * 4 + b_of(t) * 2 + zh
        rr = ratio[row_group(k)]
        for i in range(TILES):
            cols = pl.ds(i * 128, 128)
            w1 = nw[k, :, cols] - rr * gsum[k, :, cols]
            nw[k, :, cols] = w1
            land[k, mine, :, cols] = w1.astype(BF16)
        part = land.at[k, mine]
        remote(part, part, s4_send.at[k], s4_recv.at[k], high_peer).start()

    def gather_b(j, t):
        k = 2 * j + t
        wait_bytes(land.at[k, 0], s4_recv.at[k])
        part = land.at[k, pl.ds(a_of(t) * 16 + c * 8 + zl * 4 + b_of(t) * 2, 2)]
        remote(part, part, s3_send.at[k], s3_recv.at[k], b_peer(t)).start()

    def gather_low(j, t):
        k = 2 * j + t
        wait_bytes(land.at[k, pl.ds(0, 2)], s3_recv.at[k])
        part = land.at[k, pl.ds(a_of(t) * 16 + c * 8 + zl * 4, 4)]
        remote(part, part, s2_send.at[k], s2_recv.at[k], low_peer).start()

    def gather_a(j, t):
        k = 2 * j + t
        wait_bytes(land.at[k, pl.ds(0, 4)], s2_recv.at[k])
        part = land.at[k, pl.ds(a_of(t) * 16 + c * 8, 8)]
        remote(part, part, s1_send.at[k], s1_recv.at[k], a_peer(t, 1, 0)).start()
        remote(part, part, d_send.at[k], d_recv.at[k], a_peer(t, 0, 1)).start()

    def gather_core(j, t):
        k = 2 * j + t
        wait_bytes(land.at[k, pl.ds(0, 8)], s1_recv.at[k])
        part = land.at[k, pl.ds((1 - a_of(t)) * 16 + c * 8, 8)]
        remote(part, part, d_send.at[k], d_recv.at[k], a_peer(t, 0, 1)).start()

    def drain_reduce(k, carry):
        wait_bytes(land.at[k, pl.ds(0, 24)], s1_send.at[k])

        @pl.when(k >= CHUNKS - 2 * SLOTS)
        def _():
            wait_bytes(s2buf.at[k], s2_send.at[k])
        wait_bytes(s3buf.at[k], s3_send.at[k])
        wait_bytes(s4buf.at[k], s4_send.at[k])
        return carry
    lax.fori_loop(0, CHUNKS, drain_reduce, 0)

    w_low, w_high = small_totals(first_sums)
    u_low, u_high = small_totals(second_sums)
    r_low = LEARN_RATE * (jnp.sqrt(w_low) / jnp.sqrt(u_low))
    r_high = LEARN_RATE * (jnp.sqrt(w_high) / jnp.sqrt(u_high))
    r_small = jnp.concatenate([jnp.broadcast_to(r_low, (8, 128)), jnp.broadcast_to(r_high, (8, 128))], axis=1)
    new_small = small_w - r_small * u_small
    small_new[...] = new_small
    small_all[me] = new_small
    state_small[1] = m1_small
    state_small[2] = v1_small

    def small_stage(j, t):
        if t == 1:
            return

        @pl.when(j == 0)
        def _():
            to_others(me, lambda i: remote(small_new, small_all.at[me], misc_send.at[3], misc_recv.at[3], i).start())
            unpack_state(small_new[...], nw_vec, nw_wide, square)
            unpack_state(state_small[1], nm_vec, nm_wide, square)
            unpack_state(state_small[2], nv_vec, nv_wide, square)

        @pl.when(j == PAIRS - 3)
        def _():
            wait_bytes(small_all.at[pl.ds(0, GROUP - 1)], misc_recv.at[3])
            wait_bytes(small_all.at[pl.ds(0, GROUP - 1)], misc_send.at[3])
            unpack_replica(small_all, rep_vec, rep_wide)
    pipeline((gather_high, gather_b, gather_low, gather_a, gather_core, small_stage))

    def drain_gather(k, carry):
        wait_bytes(land.at[k, pl.ds(0, 16)], d_recv.at[k])
        wait_bytes(land.at[k, pl.ds(0, 16)], d_send.at[k])
        wait_bytes(land.at[k, pl.ds(0, 8)], s1_send.at[k])
        wait_bytes(land.at[k, pl.ds(0, 4)], s2_send.at[k])
        wait_bytes(land.at[k, pl.ds(0, 2)], s3_send.at[k])
        wait_bytes(land.at[k, 0], s4_send.at[k])
        return carry
    lax.fori_loop(0, CHUNKS, drain_gather, 0)


def store_kernel(land, nw, nm, nv, *refs):
    small, (rep_attn, rep_mlp, w_attn, w_mlp, m_attn, m_mlp, v_attn, v_mlp), small_out, sem = refs[:8], refs[8:16], refs[16:24], refs[24]
    state_out = ((nw, w_attn, w_mlp), (nm, m_attn, m_mlp), (nv, v_attn, v_mlp))
    for i in range(8):
        pltpu.make_async_copy(small[i], small_out[i], sem.at[4 + i]).start()

    def pair_body(j, carry):
        for t in range(2):
            k = 2 * j + t

            def issue(rep, which, own, rg, sub):
                rows = pl.ds(pl.multiple_of(rg * ROWS, ROWS), ROWS)
                base = sub * WIDTH
                for q in range(32):
                    aa, cc, zl, bb, zh = q // 16, q // 8 % 2, q // 4 % 2, q // 2 % 2, q % 2
                    owner = index_of(zh * 2 + zl, bb, aa, cc) if t == 0 else index_of(zh * 2 + zl, aa, bb, cc)
                    pltpu.make_async_copy(land.at[k, q], rep.at[rows, pl.ds(pl.multiple_of(base + owner * own, 128), WIDTH)], sem.at[0]).start()
                for i, refs in enumerate(state_out):
                    pltpu.make_async_copy(refs[0].at[k], refs[1 + which].at[rows, pl.ds(pl.multiple_of(base, 128), WIDTH)], sem.at[1 + i]).start()
            bank_of(k, lambda rg, sub: issue(rep_attn, 0, OWN_A, rg, sub), lambda rg, sub: issue(rep_mlp, 1, OWN_M, rg, sub))
        return carry
    lax.fori_loop(0, PAIRS, pair_body, 0)
    wait_bytes(land, sem.at[0])
    for i, refs in enumerate(state_out):
        wait_bytes(refs[0], sem.at[1 + i])
    for i in range(8):
        pltpu.make_async_copy(small[i], small_out[i], sem.at[4 + i]).wait()


def solution(mesh):
    grad_spec = P(AXIS, None, None)
    shard_spec = P(None, AXIS)
    full_spec = P(None, None)

    def local_step(g_attn, g_mlp, g_wide, g_vec, w_attn, w_mlp, w_wide, w_vec, m_attn, m_mlp, m_wide, m_vec, v_attn, v_mlp, v_wide, v_vec):
        hbm = pl.BlockSpec(memory_space=pl.ANY)
        vmem = pl.BlockSpec(memory_space=pltpu.VMEM)
        block = (CHUNKS, ROWS, WIDTH)
        small_shapes = [((146, 256), BF16), ((16, 1024), BF16)] + [((8, 146), F32), ((16, 32), F32)] * 3
        dma = pltpu.SemaphoreType.DMA
        land, nw, nm, nv, *small = pl.pallas_call(
            step_kernel,
            out_shape=[pltpu.VMEM((CHUNKS, 32, ROWS, WIDTH), BF16), pltpu.VMEM(block, F32), pltpu.VMEM(block, F32), pltpu.VMEM(block, F32)]
            + [pltpu.VMEM(shape, dtype) for shape, dtype in small_shapes],
            in_specs=[hbm, hbm, vmem, vmem] + [hbm] * 6 + [vmem] * 6,
            out_specs=[vmem] * 12,
            scratch_shapes=[
                pltpu.VMEM((2 * SLOTS, 8, ROWS, WIDTH), F32),
                pltpu.VMEM((CHUNKS, 4, ROWS, WIDTH), F32),
                pltpu.VMEM((CHUNKS, 2, ROWS, WIDTH), F32),
                pltpu.VMEM(block, F32),
                pltpu.VMEM(block, F32),
                pltpu.VMEM((GROUP, 8, 256), F32),
                pltpu.VMEM((GROUP, 8, 256), F32),
                pltpu.VMEM((GROUP, 8, 256), F32),
                pltpu.VMEM((8, 256), F32),
                pltpu.VMEM((3, 8, 256), F32),
                pltpu.VMEM((256, 256), F32),
                pltpu.VMEM((128, 1024), F32),
                pltpu.VMEM((8, 256), F32),
                pltpu.VMEM((128, 128), F32),
                pltpu.VMEM((2, 4, 128), F32),
                pltpu.VMEM((GROUP, 4, 128), F32),
                pltpu.VMEM((GROUP, 4, 128), F32),
                pltpu.VMEM((6, ROWS, 128), F32),
                pltpu.VMEM((6, ROWS, 128), F32),
                pltpu.VMEM((6, ROWS, 128), F32),
                pltpu.VMEM((ROWS, 128), F32),
                pltpu.VMEM((ROWS, 128), F32),
            ] + [dma((CHUNKS,))] * 10 + [dma((3,)), dma((4,)), dma((4,))],
            compiler_params=pltpu.CompilerParams(collective_id=0, has_side_effects=True, vmem_limit_bytes=30 * 1024 * 1024),
            name="lamb_step",
        )(g_attn, g_mlp, g_vec, g_wide, w_attn, w_mlp, m_attn, m_mlp, v_attn, v_mlp, w_vec.T, w_wide, m_vec.T, m_wide, v_vec.T, v_wide)
        shard_a = jax.ShapeDtypeStruct((64, OWN_A), F32)
        shard_m = jax.ShapeDtypeStruct((32, OWN_M), F32)
        (rep_attn, rep_mlp, nw_attn, nw_mlp, nm_attn, nm_mlp, nv_attn, nv_mlp,
         rep_vec, rep_wide, nw_vec, nw_wide, nm_vec, nm_wide, nv_vec, nv_wide) = pl.pallas_call(
            store_kernel,
            out_shape=[jax.ShapeDtypeStruct((64, OWN_A * GROUP), BF16), jax.ShapeDtypeStruct((32, OWN_M * GROUP), BF16),
                       shard_a, shard_m, shard_a, shard_m, shard_a, shard_m] + [jax.ShapeDtypeStruct(shape, dtype) for shape, dtype in small_shapes],
            in_specs=[vmem] * 12,
            out_specs=[hbm] * 16,
            scratch_shapes=[dma((12,))],
            compiler_params=pltpu.CompilerParams(vmem_limit_bytes=1024 * 1024),
            name="store_results",
        )(land, nw, nm, nv, *small)
        return (rep_attn, rep_mlp, rep_wide, rep_vec, nw_attn, nw_mlp, nw_wide, nw_vec.T, nm_attn, nm_mlp, nm_wide, nm_vec.T, nv_attn, nv_mlp, nv_wide, nv_vec.T)

    return jax.shard_map(local_step, mesh=mesh, in_specs=(grad_spec,) * 4 + (shard_spec,) * 12, out_specs=(full_spec,) * 4 + (shard_spec,) * 12, check_vma=False)
```

time: 424 us -> 337 us (0.79)
  Pallas kernels: 390 us -> 336 us
  local copies, waits for them, and re-layouts: 27.2 us -> 0 us
    pallas_call x2, Pallas kernels: 390 us -> 336 us  [the longest x1 326 us: local_step(): pl.pallas_call(step_kernel, out_shape=[pltpu.VMEM((CHUNKS, 32, ROWS, WIDT...]
    unnamed x18 -> x0, local copies, waits for them, and re-layouts: 22.5 us -> none
where the time goes in v2:
time: 337 us; the launch traced here: 336 us
  Pallas kernels  336 us (100%)
    pallas_call x1, Pallas kernels, local_step(): pl.pallas_call(step_kernel, out_shape=[pltpu.VMEM((CHUNKS, 32, ROWS, WIDT...  326 us
    pallas_call x1, Pallas kernels, local_step(): pl.pallas_call(store_kernel, out_shape=[jax.ShapeDtypeStruct((64, OWN_A *...  9.61 us

profile of v2, /device:TPU:0, one launch (start us, length us, event | category | flops | bytes accessed | tf_op | source)
XLA Modules:
  0.0 336.3 jit_solution(16146893342599451845)
XLA Ops:
  0.7 326.1 %lamb_step.1 = (bf16[24,32,16,1024]{3,2,1,0:T(8,128)(2,1)S(1)}, f32[24,16,1024]{2,1,0:T(8,128)S(1)}, f32[24,16,1024]{2,1,0:T(8,128)S(1)}, f32[24,16,1024]{2,1,0:...) custom-call(bf16[1,64,65536]{2,1,0:T(8,128)(2,1)} %g_attn.1, ...), custom_call_target="tpu_custom_call" | custom-call | tf_op jit(solution)/shard_map/lamb_step/pallas_call | solution.py:478
  326.7 9.6 %store_results.1 = (bf16[64,65536]{1,0:T(8,128)(2,1)}, bf16[32,262144]{1,0:T(8,128)(2,1)}, f32[64,2048]{1,0:T(8,128)}, f32[32,8192]{1,0:T(8,128)}, f32[64,2048]{...) custom-call(bf16[24,32,16,1024]{3,2,1,0:T(8,128)(2,1)S(1)} %get-tupl, ...), custom_call_target="tpu_custom_call" | custom-call | tf_op jit(solution)/shard_map/store_results/pallas_call | solution.py:514

commit v3 on v0

v3 whole, which is shorter than its diff:
```python
import jax
import jax.numpy as jnp
from jax import lax
from jax.experimental import pallas as pl
from jax.experimental.pallas import tpu as pltpu
from jax.sharding import PartitionSpec as P

STEP_NUMBER = 10
LEARN_RATE = 0.04
BETA_FIRST = 0.9
BETA_SECOND = 0.999
EPSILON = 1e-6
WEIGHT_DECAY = 0.01
MAX_NORM = 1.0
FIRST_SCALE = 1.0 / (1.0 - BETA_FIRST ** STEP_NUMBER)
SECOND_SCALE = 1.0 / (1.0 - BETA_SECOND ** STEP_NUMBER)

AXIS = "data"
MESH = pl.DeviceIdType.MESH
F32 = jnp.float32
BF16 = jnp.bfloat16
LANES = 128
SUBLANES = 8
MIB = 1024 * 1024

GROUP = 32
ROWS = 16
WIDTH = 512
OWN_A = 2048
OWN_M = 8192
SUB_A = OWN_A // WIDTH
SUB_M = OWN_M // WIDTH
CHUNKS_A = 4 * SUB_A
CHUNKS = CHUNKS_A + 2 * SUB_M
PAIRS = CHUNKS // 2
GROUPS = 6
ROW_COUNT = GROUPS * ROWS
AHEAD = 1
SLOTS = 3
TAIL = 2
HEAD = 2
REDUCE_LAGS = (0, 1, 2, 3)
GATHER_LAGS = (0, 1, 2, 3, 4, 5)
VEC_ROWS = 146
WIDE_ROWS = 16
WIDE_LANE = 64
WIDE_COLS = 32

WEIGHT = {"h": 16, "l": 8, "y": 4, "x": 2, "c": 1}
PLAIN = (("x", "l", "y"), ("y", "l", "x"))
SWAPPED = (("x", "y", "l"), ("y", "x", "l"))


def own_bits():
    me = lax.axis_index(AXIS)
    return me, {name: lax.rem(me // weight, 2) for name, weight in WEIGHT.items()}


def index_of(**bits):
    return sum(bits[name] * weight for name, weight in WEIGHT.items())


def flip(bit, other):
    return bit + other - 2 * bit * other


def remote(src, dst, send_sem, recv_sem, device):
    return pltpu.make_async_remote_copy(src_ref=src, dst_ref=dst, send_sem=send_sem, recv_sem=recv_sem, device_id=(device,), device_id_type=MESH)


def wait_bytes(ref, sem):
    pltpu.make_async_copy(ref, ref, sem).wait()


def loop(count, body, **kw):
    def step(i, carry):
        body(i)
        return carry
    lax.fori_loop(0, count, step, 0, **kw)


def tiles():
    return [pl.ds(i * LANES, LANES) for i in range(WIDTH // LANES)]


def clear(ref):
    ref[:] = jnp.zeros_like(ref)


def bank_of(k, issue):
    @pl.when(k < CHUNKS_A)
    def _():
        issue("attn", OWN_A, k // SUB_A, lax.rem(k, SUB_A))

    @pl.when(k >= CHUNKS_A)
    def _():
        local = k - CHUNKS_A
        issue("mlp", OWN_M, local // SUB_M, lax.rem(local, SUB_M))


def row_group(k):
    return jnp.where(k < CHUNKS_A, k // SUB_A, CHUNKS_A // SUB_A + (k - CHUNKS_A) // SUB_M)


def block_at(ref, rg, column):
    return ref.at[pl.ds(pl.multiple_of(rg * ROWS, ROWS), ROWS), pl.ds(pl.multiple_of(column, LANES), WIDTH)]


def adam(gs, w, m, v, clip):
    clipped = clip * gs
    new_m = BETA_FIRST * m + (1.0 - BETA_FIRST) * clipped
    new_v = BETA_SECOND * v + (1.0 - BETA_SECOND) * (clipped * clipped)
    u = (new_m * FIRST_SCALE) / (jnp.sqrt(new_v * SECOND_SCALE) + EPSILON) + WEIGHT_DECAY * w
    return u, new_m, new_v


def to_others(me, start_one):
    loop(GROUP - 1, lambda i: start_one(lax.rem(me + 1 + i, GROUP)))


def wide_shift(g):
    return WIDE_LANE + WIDE_ROWS * g


def wide_back(g):
    return (LANES - wide_shift(g)) % LANES


def rolled(x, shift):
    return pltpu.roll(x, shift, 1) if shift else x


def pack_state(vec_ref, wide_ref, flat, square, fill):
    clear(flat)
    flat[:, :VEC_ROWS] = vec_ref[:]
    clear(square)
    square[:WIDE_ROWS, :WIDE_COLS] = wide_ref[:]
    wide_t = square[:].T
    wide = sum(rolled(wide_t[SUBLANES * g:SUBLANES * (g + 1)], wide_shift(g)) for g in range(4))
    vec = flat[:]
    lane = lax.broadcasted_iota(jnp.int32, vec.shape, 1)
    packed = jnp.concatenate([vec[:, :LANES], vec[:, LANES:] + wide], axis=1)
    return jnp.where(jnp.logical_and(lane >= VEC_ROWS, lane < LANES + WIDE_LANE), fill, packed)


def unpack_state(packed, vec_ref, wide_ref, square):
    vec_ref[:] = packed[:, :VEC_ROWS]
    clear(square)
    for g in range(4):
        square[SUBLANES * g:SUBLANES * (g + 1), :] = rolled(packed[:, LANES:], wide_back(g))
    wide_ref[:] = square[:].T[:WIDE_ROWS, :WIDE_COLS]


def pack_grads(g_vec, g_wide, g_small, big, long):
    clear(big)
    big[:VEC_ROWS, :] = g_vec[0].astype(F32)
    clear(long)
    long[:WIDE_ROWS, :] = g_wide[0].astype(F32)
    vec = big[:].T
    wide_t = long[:].T.reshape(GROUP, 4, SUBLANES, LANES)
    wide = sum(rolled(wide_t[:, g].reshape(GROUP * SUBLANES, LANES), wide_shift(g)) for g in range(4))
    g_small[:, :, :LANES] = vec[:, :LANES].reshape(GROUP, SUBLANES, LANES).astype(BF16)
    g_small[:, :, LANES:] = (vec[:, LANES:] + wide).reshape(GROUP, SUBLANES, LANES).astype(BF16)


def unpack_replica(small_all, rep_vec, rep_wide):
    rep_vec[:] = small_all[:].astype(F32).reshape(GROUP * SUBLANES, 2 * LANES).T[:VEC_ROWS].astype(BF16)
    upper = small_all[:, :, LANES:].astype(F32).reshape(GROUP * SUBLANES, LANES)
    parts = [rolled(upper, wide_back(g)).reshape(GROUP, 1, SUBLANES, LANES) for g in range(4)]
    rep_wide[:] = jnp.concatenate(parts, axis=1).reshape(GROUP * WIDE_COLS, LANES).T[:WIDE_ROWS].astype(BF16)


def step_kernel(g_attn, g_mlp, g_vec, g_wide, w_attn, w_mlp, m_attn, m_mlp, v_attn, v_mlp, w_vec, w_wide, m_vec, m_wide, v_vec, v_wide,
                land, nw, nm, nv, rep_vec, rep_wide, nw_vec, nw_wide, nm_vec, nm_wide, nv_vec, nv_wide,
                acc1, s2buf, s3buf, s4buf, gsum, g_small, small_in, small_all, small_new, state_small, big, long, flat, square,
                msg, inboxes, rows_w, rows_u, ratio, clip_tile, n_acc,
                s1_send, s1_recv, s2_send, s2_recv, s3_send, s3_recv, s4_send, s4_recv, d_send, d_recv, load_sem, misc_send, misc_recv):
    me, bits = own_bits()
    grads = {"attn": g_attn, "mlp": g_mlp}
    states = {"attn": (w_attn, m_attn, v_attn), "mlp": (w_mlp, m_mlp, v_mlp)}

    def peer(name):
        return index_of(**{**bits, name: 1 - bits[name]})

    barrier = pltpu.get_barrier_semaphore()
    to_others(me, lambda i: pl.semaphore_signal(barrier, inc=1, device_id=(i,), device_id_type=MESH))

    def load_state(k):
        def issue(bank, own, rg, sub):
            for i, dst in enumerate((nw, nm, nv)):
                pltpu.make_async_copy(block_at(states[bank][i], rg, sub * WIDTH), dst.at[k], load_sem.at[i]).start()
        bank_of(k, issue)
    loop(CHUNKS, load_state)
    pack_grads(g_vec, g_wide, g_small, big, long)

    pl.semaphore_wait(barrier, GROUP - 1)

    def first_start(j, t, order):
        k = 2 * j + t
        one, two, three = order

        def issue(bank, own, rg, sub):
            def body(b):
                for da in range(2):
                    for dc in range(2):
                        target = {one: flip(bits[one], da), "c": flip(bits["c"], dc)}
                        owner = index_of(**target, **{two: b // 4, three: lax.rem(b // 2, 2), "h": lax.rem(b, 2)})
                        src = block_at(grads[bank].at[0], rg, owner * own + sub * WIDTH)
                        dst = land.at[k, (da * 2 + dc) * 8 + b]
                        if da or dc:
                            remote(src, dst, s1_send.at[k], s1_recv.at[k], index_of(**{**bits, **target})).start()
                        else:
                            pltpu.make_async_copy(src, dst, s1_recv.at[k]).start()
            loop(8, body)
        bank_of(k, issue)

    def first_finish(j, t, order):
        k = 2 * j + t
        slot = lax.rem(j, SLOTS) * 2 + t

        @pl.when(j >= SLOTS)
        def _():
            wait_bytes(s2buf.at[k - 2 * SLOTS], s2_send.at[k - 2 * SLOTS])
        wait_bytes(land.at[k], s1_recv.at[k])

        def body(b):
            for cols in tiles():
                own, core, far, both = [land[k, p * 8 + b, :, cols].astype(F32) for p in range(4)]
                acc1[slot, b, :, cols] = (own + core) + (far + both)
        loop(8, body)
        remote(acc1.at[slot, pl.ds((1 - bits[order[1]]) * 4, 4)], s2buf.at[k], s2_send.at[k], s2_recv.at[k], peer(order[1])).start()

    def second_finish(j, t, order):
        k = 2 * j + t
        slot = lax.rem(j, SLOTS) * 2 + t
        two, three = bits[order[1]], bits[order[2]]
        wait_bytes(s2buf.at[k], s2_recv.at[k])

        def body(b):
            for cols in tiles():
                s2buf[k, b, :, cols] = s2buf[k, b, :, cols] + acc1[slot, two * 4 + b, :, cols]
        loop(4, body)
        remote(s2buf.at[k, pl.ds((1 - three) * 2, 2)], s3buf.at[k], s3_send.at[k], s3_recv.at[k], peer(order[2])).start()

    def third_finish(j, t, order):
        k = 2 * j + t
        wait_bytes(s3buf.at[k], s3_recv.at[k])
        for b in range(2):
            for cols in tiles():
                s3buf[k, b, :, cols] = s3buf[k, b, :, cols] + s2buf[k, bits[order[2]] * 2 + b, :, cols]
        remote(s3buf.at[k, 1 - bits["h"]], s4buf.at[k], s4_send.at[k], s4_recv.at[k], peer("h")).start()

    def fourth_finish(j, t, order):
        k = 2 * j + t
        wait_bytes(s4buf.at[k], s4_recv.at[k])
        total = n_acc[:]
        for cols in tiles():
            gs = (s3buf[k, bits["h"], :, cols] + s4buf[k, :, cols]) * (1.0 / GROUP)
            gsum[k, :, cols] = gs
            total = total + gs * gs
        n_acc[:] = total

    def pair(stage, j, plain):
        for orders, chosen in ((PLAIN, plain), (SWAPPED, jnp.logical_not(plain))):
            @pl.when(chosen)
            def _():
                for t, order in enumerate(orders):
                    stage(j, t, order)

    for j in range(AHEAD):
        for t, order in enumerate(PLAIN):
            first_start(j, t, order)

    to_others(me, lambda i: remote(g_small.at[i], small_in.at[me], misc_send.at[0], misc_recv.at[0], i).start())
    small_in[me] = g_small[me]

    for i, (vec_ref, wide_ref, fill) in enumerate(((w_vec, w_wide, 1.0), (m_vec, m_wide, 0.0), (v_vec, v_wide, 1.0))):
        state_small[i] = pack_state(vec_ref, wide_ref, flat, square, fill)
    for i, ref in enumerate((nw, nm, nv)):
        wait_bytes(ref, load_sem.at[i])
    clear(n_acc)
    clear(rows_w)
    clear(rows_u)

    def weight_squares(k):
        total = rows_w[row_group(k)]
        for cols in tiles():
            w = nw[k, :, cols]
            total = total + w * w
        rows_w[row_group(k)] = total
    loop(CHUNKS, weight_squares)

    def reduce_step(j):
        @pl.when(j + AHEAD < PAIRS)
        def _():
            pair(first_start, j + AHEAD, j + AHEAD < PAIRS - TAIL)
        for lag, stage in zip(REDUCE_LAGS, (first_finish, second_finish, third_finish, fourth_finish)):
            @pl.when(jnp.logical_and(j >= lag, j < PAIRS + lag))
            def _():
                pair(stage, j - lag, j - lag < PAIRS - TAIL)
    loop(PAIRS + max(REDUCE_LAGS), reduce_step)

    wait_bytes(small_in.at[:GROUP - 1], misc_recv.at[0])
    wait_bytes(small_in.at[:GROUP - 1], misc_send.at[0])
    gs_small = jnp.sum(small_in[:].astype(F32), axis=0) * (1.0 / GROUP)

    sub_iota = lax.broadcasted_iota(jnp.int32, msg.shape[1:], 0)
    square_shape = (ROW_COUNT, LANES)
    eye = lax.broadcasted_iota(jnp.int32, square_shape, 0) == lax.broadcasted_iota(jnp.int32, square_shape, 1)

    def to_row(column_parts):
        sums = jnp.sum(column_parts, axis=1, keepdims=True)
        return jnp.sum(jnp.where(eye, jnp.broadcast_to(sums, square_shape), 0.0), axis=0, keepdims=True)

    def halves(small):
        sums = jnp.sum(small, axis=0, keepdims=True)
        return sums[:, :LANES], sums[:, LANES:]

    def sum_over_devices(rows, slot):
        inbox = inboxes.at[slot]
        value = sum(jnp.where(sub_iota == i, jnp.broadcast_to(row, sub_iota.shape), 0.0) for i, row in enumerate(rows))
        msg[slot] = value
        inbox[me] = value
        to_others(me, lambda i: remote(msg.at[slot], inbox.at[me], misc_send.at[1 + slot], misc_recv.at[1 + slot], i).start())
        wait_bytes(inbox.at[:GROUP - 1], misc_recv.at[1 + slot])
        wait_bytes(inbox.at[:GROUP - 1], misc_send.at[1 + slot])
        total = jnp.sum(inbox[:], axis=0)
        return [total[i:i + 1] for i in range(4)]

    small_w = state_small[0]
    low, high = halves(gs_small * gs_small)
    square_row = jnp.sum(n_acc[:], axis=0, keepdims=True) + low + high
    w_large, w_low, w_high, squares = sum_over_devices((to_row(rows_w[:].reshape(square_shape)), *halves(small_w * small_w), square_row), 0)
    clip = jnp.minimum(1.0, MAX_NORM / jnp.sqrt(jnp.sum(squares, axis=1, keepdims=True)))
    clip_tile[:] = jnp.broadcast_to(clip, clip_tile.shape)

    def direction(k):
        cl = clip_tile[:]
        total = rows_u[row_group(k)]
        for cols in tiles():
            u, m1, v1 = adam(gsum[k, :, cols], nw[k, :, cols], nm[k, :, cols], nv[k, :, cols], cl)
            nm[k, :, cols] = m1
            nv[k, :, cols] = v1
            gsum[k, :, cols] = u
            total = total + u * u
        rows_u[row_group(k)] = total
    loop(CHUNKS, direction)
    u_small, m1_small, v1_small = adam(gs_small, small_w, state_small[1], state_small[2], jnp.broadcast_to(clip, small_w.shape))
    u_large, u_low, u_high, _ = sum_over_devices((to_row(rows_u[:].reshape(square_shape)), *halves(u_small * u_small)), 1)

    ratio_row = jnp.sqrt(w_large) / jnp.sqrt(u_large)
    ratio_col = jnp.sum(jnp.where(eye, jnp.broadcast_to(ratio_row, square_shape), 0.0), axis=1, keepdims=True)
    ratio[:] = jnp.broadcast_to(LEARN_RATE * ratio_col, square_shape).reshape(ratio.shape)

    lane = lax.broadcasted_iota(jnp.int32, (1, LANES), 1)

    def small_ratio(w_sums, u_sums):
        return jnp.broadcast_to(LEARN_RATE * (jnp.sqrt(w_sums) / jnp.sqrt(u_sums)), (SUBLANES, LANES))

    def with_wide_totals(upper):
        wide = jnp.where(lane >= WIDE_LANE, upper, 0.0)
        for shift in (64, 32, 16):
            wide = wide + rolled(wide, shift)
        return jnp.where(lane >= WIDE_LANE, wide, upper)

    def span(k, order, depth):
        names = (order[0], "c", order[1], order[2], "h")[:depth]
        size = GROUP >> depth
        start = sum(bits[name] * (GROUP >> (i + 1)) for i, name in enumerate(names))
        return land.at[k, pl.ds(start, size)]

    def gather_high(j, t, order):
        k = 2 * j + t
        mine = span(k, order, 5)
        rr = ratio[row_group(k)]
        for cols in tiles():
            w1 = nw[k, :, cols] - rr * gsum[k, :, cols]
            nw[k, :, cols] = w1
            mine[0, :, cols] = w1.astype(BF16)
        remote(mine, mine, s4_send.at[k], s4_recv.at[k], peer("h")).start()

    def gather_three(j, t, order):
        k = 2 * j + t
        wait_bytes(land.at[k, :1], s4_recv.at[k])
        part = span(k, order, 4)
        remote(part, part, s3_send.at[k], s3_recv.at[k], peer(order[2])).start()

    def gather_two(j, t, order):
        k = 2 * j + t
        wait_bytes(land.at[k, :2], s3_recv.at[k])
        part = span(k, order, 3)
        remote(part, part, s2_send.at[k], s2_recv.at[k], peer(order[1])).start()

    def gather_one(j, t, order):
        k = 2 * j + t
        wait_bytes(land.at[k, :4], s2_recv.at[k])
        part = span(k, order, 2)
        remote(part, part, s1_send.at[k], s1_recv.at[k], peer(order[0])).start()
        remote(part, part, d_send.at[k], d_recv.at[k], peer("c")).start()

    def gather_core(j, t, order):
        k = 2 * j + t
        wait_bytes(land.at[k, :8], s1_recv.at[k])
        part = land.at[k, pl.ds((1 - bits[order[0]]) * 16 + bits["c"] * 8, 8)]
        remote(part, part, d_send.at[k], d_recv.at[k], peer("c")).start()

    def drain_reduce(k):
        wait_bytes(land.at[k, :24], s1_send.at[k])

        @pl.when(k >= CHUNKS - 2 * SLOTS)
        def _():
            wait_bytes(s2buf.at[k], s2_send.at[k])
        wait_bytes(s3buf.at[k], s3_send.at[k])
        wait_bytes(s4buf.at[k], s4_send.at[k])
    loop(CHUNKS, drain_reduce)

    r_small = jnp.concatenate([small_ratio(w_low, u_low), small_ratio(with_wide_totals(w_high), with_wide_totals(u_high))], axis=1)
    state_small[0] = small_w - r_small * u_small
    state_small[1] = m1_small
    state_small[2] = v1_small
    small_new[:] = state_small[0].astype(BF16)
    small_all[me] = small_new[:]

    def gather_step(j):
        for lag, stage in zip(GATHER_LAGS, (gather_high, gather_three, gather_two, gather_one, gather_core)):
            @pl.when(jnp.logical_and(j >= lag, j < PAIRS + lag))
            def _():
                pair(stage, j - lag, j - lag >= HEAD)

        @pl.when(j == 4)
        def _():
            to_others(me, lambda i: remote(small_new, small_all.at[me], misc_send.at[3], misc_recv.at[3], i).start())
            for i, refs in enumerate(((nw_vec, nw_wide), (nm_vec, nm_wide), (nv_vec, nv_wide))):
                unpack_state(state_small[i], *refs, square)

        @pl.when(j == PAIRS)
        def _():
            wait_bytes(small_all.at[:GROUP - 1], misc_recv.at[3])
            wait_bytes(small_all.at[:GROUP - 1], misc_send.at[3])
            unpack_replica(small_all, rep_vec, rep_wide)
    loop(PAIRS + max(GATHER_LAGS), gather_step)

    def drain_gather(k):
        for size, sem in ((16, d_recv), (16, d_send), (8, s1_send), (4, s2_send), (2, s3_send), (1, s4_send)):
            wait_bytes(land.at[k, :size], sem.at[k])
    loop(CHUNKS, drain_gather)


def store_kernel(land, nw, nm, nv, *refs):
    small, large_out, small_out, sem = refs[:8], refs[8:16], refs[16:24], refs[24]
    outs = {"attn": large_out[::2], "mlp": large_out[1::2]}
    for i in range(8):
        pltpu.make_async_copy(small[i], small_out[i], sem.at[4 + i]).start()

    def store_pair(j, orders):
        for t, order in enumerate(orders):
            k = 2 * j + t

            def issue(bank, own, rg, sub):
                base = sub * WIDTH
                for q in range(GROUP):
                    names = (order[0], "c", order[1], order[2], "h")
                    owner = index_of(**{name: q * (2 << i) // GROUP % 2 for i, name in enumerate(names)})
                    pltpu.make_async_copy(land.at[k, q], block_at(outs[bank][0], rg, base + owner * own), sem.at[0]).start()
                for i, ref in enumerate((nw, nm, nv)):
                    pltpu.make_async_copy(ref.at[k], block_at(outs[bank][1 + i], rg, base), sem.at[1 + i]).start()
            bank_of(k, issue)
    loop(HEAD, lambda j: store_pair(j, SWAPPED))
    loop(PAIRS - HEAD, lambda j: store_pair(j + HEAD, PLAIN))
    wait_bytes(land, sem.at[0])
    for i, ref in enumerate((nw, nm, nv)):
        wait_bytes(ref, sem.at[1 + i])
    for i in range(8):
        pltpu.make_async_copy(small[i], small_out[i], sem.at[4 + i]).wait()


def solution(mesh):
    grad_spec = P(AXIS, None, None)
    shard_spec = P(None, AXIS)
    full_spec = P(None, None)
    hbm = pl.BlockSpec(memory_space=pl.ANY)
    in_vmem = pl.BlockSpec(memory_space=pltpu.VMEM)
    vmem, dma = pltpu.VMEM, pltpu.SemaphoreType.DMA
    block = (CHUNKS, ROWS, WIDTH)
    packed = (SUBLANES, 2 * LANES)
    small_shapes = [((VEC_ROWS, OWN_M // GROUP), BF16), ((WIDE_ROWS, WIDE_COLS * GROUP), BF16)] + [((SUBLANES, VEC_ROWS), F32), ((WIDE_ROWS, WIDE_COLS), F32)] * 3

    def local_step(g_attn, g_mlp, g_wide, g_vec, w_attn, w_mlp, w_wide, w_vec, m_attn, m_mlp, m_wide, m_vec, v_attn, v_mlp, v_wide, v_vec):
        scratch = [vmem((2 * SLOTS, 8, ROWS, WIDTH), F32), vmem((CHUNKS, 4, ROWS, WIDTH), F32), vmem((CHUNKS, 2, ROWS, WIDTH), F32), vmem(block, F32), vmem(block, F32)]
        scratch += [vmem((GROUP, *packed), BF16)] * 3 + [vmem(packed, BF16), vmem((3, *packed), F32)]
        scratch += [vmem((2 * LANES, GROUP * SUBLANES), F32), vmem((LANES, GROUP * WIDE_COLS), F32), vmem(packed, F32), vmem((LANES, LANES), F32)]
        scratch += [vmem((2, 4, LANES), F32), vmem((2, GROUP, 4, LANES), F32)] + [vmem((GROUPS, ROWS, LANES), F32)] * 3 + [vmem((ROWS, LANES), F32)] * 2
        scratch += [dma((CHUNKS,))] * 10 + [dma((3,)), dma((4,)), dma((4,))]
        results = pl.pallas_call(
            step_kernel,
            out_shape=[vmem((CHUNKS, GROUP, ROWS, WIDTH), BF16)] + [vmem(block, F32)] * 3 + [vmem(*item) for item in small_shapes],
            in_specs=[hbm] * 2 + [in_vmem] * 2 + [hbm] * 6 + [in_vmem] * 6,
            out_specs=[in_vmem] * 12,
            scratch_shapes=scratch,
            compiler_params=pltpu.CompilerParams(collective_id=0, has_side_effects=True, vmem_limit_bytes=30 * MIB),
            name="lamb_step",
        )(g_attn, g_mlp, g_vec, g_wide, w_attn, w_mlp, m_attn, m_mlp, v_attn, v_mlp, w_vec.T, w_wide, m_vec.T, m_wide, v_vec.T, v_wide)
        shards = [jax.ShapeDtypeStruct(w_attn.shape, F32), jax.ShapeDtypeStruct(w_mlp.shape, F32)] * 3
        (rep_attn, rep_mlp, nw_attn, nw_mlp, nm_attn, nm_mlp, nv_attn, nv_mlp,
         rep_vec, rep_wide, nw_vec, nw_wide, nm_vec, nm_wide, nv_vec, nv_wide) = pl.pallas_call(
            store_kernel,
            out_shape=[jax.ShapeDtypeStruct(g_attn.shape[1:], BF16), jax.ShapeDtypeStruct(g_mlp.shape[1:], BF16)] + shards + [jax.ShapeDtypeStruct(*item) for item in small_shapes],
            in_specs=[in_vmem] * 12,
            out_specs=[hbm] * 16,
            scratch_shapes=[dma((12,))],
            compiler_params=pltpu.CompilerParams(vmem_limit_bytes=MIB),
            name="store_results",
        )(*results)
        return (rep_attn, rep_mlp, rep_wide, rep_vec, nw_attn, nw_mlp, nw_wide, nw_vec.T, nm_attn, nm_mlp, nm_wide, nm_vec.T, nv_attn, nv_mlp, nv_wide, nv_vec.T)

    return jax.shard_map(local_step, mesh=mesh, in_specs=(grad_spec,) * 4 + (shard_spec,) * 12, out_specs=(full_spec,) * 4 + (shard_spec,) * 12, check_vma=False)
```

time: 931 us -> 322 us (0.35)
  waiting for transfers between devices: 596 us -> 0 us
  Pallas kernels: 0 us -> 321 us
  blocking collectives: 175 us -> 0 us
  local copies, waits for them, and re-layouts: 86.8 us -> 0 us
  starting transfers between devices: 28.3 us -> 0 us
  other arithmetic: 27.1 us -> 0 us
  between operations: 17.6 us -> 0.66 us
    all_to_all x4 -> x0, waiting for transfers between devices: 485 us -> none  [local_step(): received = lax.all_to_all(by_owner, 'data', 1, 1, tiled=True)]
    pallas_call x0 -> x2, Pallas kernels: none -> 321 us  [the longest x1 311 us: local_step(): pl.pallas_call(step_kernel, out_shape=[vmem((CHUNKS, GROUP, ROWS, WIDTH),...]
    all_gather x2 -> x0, waiting for transfers between devices: 110 us -> none  [local_step(): lax.all_gather(new_weight.astype(jnp.bfloat16), 'data', axis=1, tiled=True)]
    psum x2 -> x0, blocking collectives: 96.6 us -> none  [the longest x1 54.4 us: local_step(): lax.psum(local_square, 'data')]
    all_gather x2 -> x0, blocking collectives: 77.9 us -> none  [local_step(): lax.all_gather(new_weight.astype(jnp.bfloat16), 'data', axis=1, tiled=True)]
    unnamed x37 -> x0, local copies, waits for them, and re-layouts: 52.2 us -> none
    reshape x4 -> x0, local copies, waits for them, and re-layouts: 34.4 us -> none  [local_step(): by_owner = grad_bank.reshape(row_count, group_size, shard_width)]
    all_to_all x4 -> x0, starting transfers between devices: 28 us -> none  [local_step(): received = lax.all_to_all(by_owner, 'data', 1, 1, tiled=True)]
  transfers between devices with their start and end apart: 6 -> 0, of which waited for: 4 -> 0; matrix products, arithmetic and copies ran while one was open for 8% -> 0% of each run, Pallas kernels for 0% -> 0%
where the time goes in v3:
time: 322 us
  Pallas kernels  321 us (100%)
    pallas_call x1, Pallas kernels, local_step(): pl.pallas_call(step_kernel, out_shape=[vmem((CHUNKS, GROUP, ROWS, WIDTH),...  311 us
    pallas_call x1, Pallas kernels, local_step(): pl.pallas_call(store_kernel, out_shape=[jax.ShapeDtypeStruct(g_attn.shape...  9.57 us

profile of v3, /device:TPU:0, one launch (start us, length us, event | category | flops | bytes accessed | tf_op | source)
XLA Modules:
  0.0 321.7 jit_solution(304913883191613962)
XLA Ops:
  0.7 311.5 %lamb_step.1 = (bf16[48,32,16,512]{3,2,1,0:T(8,128)(2,1)S(1)}, f32[48,16,512]{2,1,0:T(8,128)S(1)}, f32[48,16,512]{2,1,0:T(8,128)S(1)}, f32[48,16,512]{2,1,0:T(8,...) custom-call(bf16[1,64,65536]{2,1,0:T(8,128)(2,1)} %g_attn.1, ...), custom_call_target="tpu_custom_call" | custom-call | tf_op jit(solution)/shard_map/lamb_step/pallas_call | solution.py:494
  312.1 9.6 %store_results.1 = (bf16[64,65536]{1,0:T(8,128)(2,1)}, bf16[32,262144]{1,0:T(8,128)(2,1)}, f32[64,2048]{1,0:T(8,128)}, f32[32,8192]{1,0:T(8,128)}, f32[64,2048]{...) custom-call(bf16[48,32,16,512]{3,2,1,0:T(8,128)(2,1)S(1)} %get-tuple, ...), custom_call_target="tpu_custom_call" | custom-call | tf_op jit(solution)/shard_map/store_results/pallas_call | solution.py:505

commit v4 on v3

--- a/solution.py
+++ b/solution.py
@@ -37,10 +37,10 @@
 ROW_COUNT = GROUPS * ROWS
 AHEAD = 1
 SLOTS = 3
-TAIL = 2
-HEAD = 2
-REDUCE_LAGS = (0, 1, 2, 3)
-GATHER_LAGS = (0, 1, 2, 3, 4, 5)
+TAIL = 1
+HEAD = 1
+REDUCE_LAGS = (0, 1, 2, 3, 4)
+GATHER_LAGS = (0, 1, 3, 5, 8, 9)
 VEC_ROWS = 146
 WIDE_ROWS = 16
 WIDE_LANE = 64
@@ -48,7 +48,7 @@
 
 WEIGHT = {"h": 16, "l": 8, "y": 4, "x": 2, "c": 1}
 PLAIN = (("x", "l", "y"), ("y", "l", "x"))
-SWAPPED = (("x", "y", "l"), ("y", "x", "l"))
+SWAPPED = (("x", "l", "y"), ("y", "x", "l"))
 
 
 def own_bits():
@@ -190,8 +190,6 @@
             for i, dst in enumerate((nw, nm, nv)):
                 pltpu.make_async_copy(block_at(states[bank][i], rg, sub * WIDTH), dst.at[k], load_sem.at[i]).start()
         bank_of(k, issue)
-    loop(CHUNKS, load_state)
-    pack_grads(g_vec, g_wide, g_small, big, long)
 
     pl.semaphore_wait(barrier, GROUP - 1)
 
@@ -260,6 +258,16 @@
             total = total + gs * gs
         n_acc[:] = total
 
+    def reduce_done(j, t, order):
+        k = 2 * j + t
+        wait_bytes(land.at[k, :24], s1_send.at[k])
+
+        @pl.when(j >= PAIRS - SLOTS)
+        def _():
+            wait_bytes(s2buf.at[k], s2_send.at[k])
+        wait_bytes(s3buf.at[k], s3_send.at[k])
+        wait_bytes(s4buf.at[k], s4_send.at[k])
+
     def pair(stage, j, plain):
         for orders, chosen in ((PLAIN, plain), (SWAPPED, jnp.logical_not(plain))):
             @pl.when(chosen)
@@ -271,6 +279,9 @@
         for t, order in enumerate(PLAIN):
             first_start(j, t, order)
 
+    loop(CHUNKS, load_state)
+
+    pack_grads(g_vec, g_wide, g_small, big, long)
     to_others(me, lambda i: remote(g_small.at[i], small_in.at[me], misc_send.at[0], misc_recv.at[0], i).start())
     small_in[me] = g_small[me]
 
@@ -294,7 +305,7 @@
         @pl.when(j + AHEAD < PAIRS)
         def _():
             pair(first_start, j + AHEAD, j + AHEAD < PAIRS - TAIL)
-        for lag, stage in zip(REDUCE_LAGS, (first_finish, second_finish, third_finish, fourth_finish)):
+        for lag, stage in zip(REDUCE_LAGS, (first_finish, second_finish, third_finish, fourth_finish, reduce_done)):
             @pl.when(jnp.logical_and(j >= lag, j < PAIRS + lag))
             def _():
                 pair(stage, j - lag, j - lag < PAIRS - TAIL)
@@ -404,15 +415,11 @@
         part = land.at[k, pl.ds((1 - bits[order[0]]) * 16 + bits["c"] * 8, 8)]
         remote(part, part, d_send.at[k], d_recv.at[k], peer("c")).start()
 
-    def drain_reduce(k):
-        wait_bytes(land.at[k, :24], s1_send.at[k])
-
-        @pl.when(k >= CHUNKS - 2 * SLOTS)
-        def _():
-            wait_bytes(s2buf.at[k], s2_send.at[k])
-        wait_bytes(s3buf.at[k], s3_send.at[k])
-        wait_bytes(s4buf.at[k], s4_send.at[k])
-    loop(CHUNKS, drain_reduce)
+
+    def gather_done(j, t, order):
+        k = 2 * j + t
+        for size, sem in ((16, d_recv), (16, d_send), (8, s1_send), (4, s2_send), (2, s3_send), (1, s4_send)):
+            wait_bytes(land.at[k, :size], sem.at[k])
 
     r_small = jnp.concatenate([small_ratio(w_low, u_low), small_ratio(with_wide_totals(w_high), with_wide_totals(u_high))], axis=1)
     state_small[0] = small_w - r_small * u_small
@@ -422,7 +429,7 @@
     small_all[me] = small_new[:]
 
     def gather_step(j):
-        for lag, stage in zip(GATHER_LAGS, (gather_high, gather_three, gather_two, gather_one, gather_core)):
+        for lag, stage in zip(GATHER_LAGS, (gather_high, gather_three, gather_two, gather_one, gather_core, gather_done)):
             @pl.when(jnp.logical_and(j >= lag, j < PAIRS + lag))
             def _():
                 pair(stage, j - lag, j - lag >= HEAD)
@@ -439,11 +446,6 @@
             wait_bytes(small_all.at[:GROUP - 1], misc_send.at[3])
             unpack_replica(small_all, rep_vec, rep_wide)
     loop(PAIRS + max(GATHER_LAGS), gather_step)
-
-    def drain_gather(k):
-        for size, sem in ((16, d_recv), (16, d_send), (8, s1_send), (4, s2_send), (2, s3_send), (1, s4_send)):
-            wait_bytes(land.at[k, :size], sem.at[k])
-    loop(CHUNKS, drain_gather)
 
 
 def store_kernel(land, nw, nm, nv, *refs):

time: 322 us -> 313 us (0.972)
  Pallas kernels: 321 us -> 311 us
    pallas_call x1, Pallas kernels: 311 us -> 302 us  [local_step(): pl.pallas_call(step_kernel, out_shape=[vmem((CHUNKS, GROUP, ROWS, WIDTH),...]
where the time goes in v4:
time: 313 us; the launch traced here: 312 us
  Pallas kernels  311 us (99%)
    pallas_call x1, Pallas kernels, local_step(): pl.pallas_call(step_kernel, out_shape=[vmem((CHUNKS, GROUP, ROWS, WIDTH),...  302 us
    pallas_call x1, Pallas kernels, local_step(): pl.pallas_call(store_kernel, out_shape=[jax.ShapeDtypeStruct(g_attn.shape...  9.57 us

profile of v4, /device:TPU:0, one launch (start us, length us, event | category | flops | bytes accessed | tf_op | source)
XLA Modules:
  0.0 312.1 jit_solution(16387081765257208988)
XLA Ops:
  0.7 301.8 %lamb_step.1 = (bf16[48,32,16,512]{3,2,1,0:T(8,128)(2,1)S(1)}, f32[48,16,512]{2,1,0:T(8,128)S(1)}, f32[48,16,512]{2,1,0:T(8,128)S(1)}, f32[48,16,512]{2,1,0:T(8,...) custom-call(bf16[1,64,65536]{2,1,0:T(8,128)(2,1)} %g_attn.1, ...), custom_call_target="tpu_custom_call" | custom-call | tf_op jit(solution)/shard_map/lamb_step/pallas_call | solution.py:496
  302.5 9.6 %store_results.1 = (bf16[64,65536]{1,0:T(8,128)(2,1)}, bf16[32,262144]{1,0:T(8,128)(2,1)}, f32[64,2048]{1,0:T(8,128)}, f32[32,8192]{1,0:T(8,128)}, f32[64,2048]{...) custom-call(bf16[48,32,16,512]{3,2,1,0:T(8,128)(2,1)S(1)} %get-tuple, ...), custom_call_target="tpu_custom_call" | custom-call | tf_op jit(solution)/shard_map/store_results/pallas_call | solution.py:507

commit v5 on v4

--- a/solution.py
+++ b/solution.py
@@ -40,7 +40,7 @@
 TAIL = 1
 HEAD = 1
 REDUCE_LAGS = (0, 1, 2, 3, 4)
-GATHER_LAGS = (0, 1, 3, 5, 8, 9)
+GATHER_LAGS = (0, 1, 3, 5, 7, 8)
 VEC_ROWS = 146
 WIDE_ROWS = 16
 WIDE_LANE = 64
@@ -115,7 +115,7 @@
 
 
 def to_others(me, start_one):
-    loop(GROUP - 1, lambda i: start_one(lax.rem(me + 1 + i, GROUP)))
+    loop(GROUP - 1, lambda i: start_one(lax.rem(me + 1 + i, GROUP)), unroll=True)
 
 
 def wide_shift(g):
@@ -334,7 +334,6 @@
         inbox[me] = value
         to_others(me, lambda i: remote(msg.at[slot], inbox.at[me], misc_send.at[1 + slot], misc_recv.at[1 + slot], i).start())
         wait_bytes(inbox.at[:GROUP - 1], misc_recv.at[1 + slot])
-        wait_bytes(inbox.at[:GROUP - 1], misc_send.at[1 + slot])
         total = jnp.sum(inbox[:], axis=0)
         return [total[i:i + 1] for i in range(4)]
 
@@ -446,6 +445,8 @@
             wait_bytes(small_all.at[:GROUP - 1], misc_send.at[3])
             unpack_replica(small_all, rep_vec, rep_wide)
     loop(PAIRS + max(GATHER_LAGS), gather_step)
+    for slot in range(2):
+        wait_bytes(inboxes.at[slot, :GROUP - 1], misc_send.at[1 + slot])
 
 
 def store_kernel(land, nw, nm, nv, *refs):

time: 313 us -> 313 us (level)
  no operation moved by 1% of the time
where the time goes in v5:
time: 313 us; the launch traced here: 312 us
  Pallas kernels  311 us (99%)
    pallas_call x1, Pallas kernels, local_step(): pl.pallas_call(step_kernel, out_shape=[vmem((CHUNKS, GROUP, ROWS, WIDTH),...  301 us
    pallas_call x1, Pallas kernels, local_step(): pl.pallas_call(store_kernel, out_shape=[jax.ShapeDtypeStruct(g_attn.shape...  9.57 us

profile of v5, /device:TPU:0, one launch (start us, length us, event | category | flops | bytes accessed | tf_op | source)
XLA Modules:
  0.0 311.7 jit_solution(935528887973487119)
XLA Ops:
  0.7 301.5 %lamb_step.1 = (bf16[48,32,16,512]{3,2,1,0:T(8,128)(2,1)S(1)}, f32[48,16,512]{2,1,0:T(8,128)S(1)}, f32[48,16,512]{2,1,0:T(8,128)S(1)}, f32[48,16,512]{2,1,0:T(8,...) custom-call(bf16[1,64,65536]{2,1,0:T(8,128)(2,1)} %g_attn.1, ...), custom_call_target="tpu_custom_call" | custom-call | tf_op jit(solution)/shard_map/lamb_step/pallas_call | solution.py:497
  302.1 9.6 %store_results.1 = (bf16[64,65536]{1,0:T(8,128)(2,1)}, bf16[32,262144]{1,0:T(8,128)(2,1)}, f32[64,2048]{1,0:T(8,128)}, f32[32,8192]{1,0:T(8,128)}, f32[64,2048]{...) custom-call(bf16[48,32,16,512]{3,2,1,0:T(8,128)(2,1)S(1)} %get-tuple, ...), custom_call_target="tpu_custom_call" | custom-call | tf_op jit(solution)/shard_map/store_results/pallas_call | solution.py:508
